TPU v7x, 512 devices: a whole 4x8x8 slice. The times are simulated.
512 devices in a mesh: row: 32 (over z, x_lo, core), col: 16 (over y, x_hi).
Axes of the slice: x: 4 (x_hi: 2, x_lo: 2; x = x_hi * 2 + x_lo), y: 8, z: 8, core: 2. Of those that a mesh axis runs over, the one named last changes fastest.
Arguments:
- substrate: float32 [4096, 4096], P('row', 'col'), may hold values from 0.05 to 0.95
- activator: float32 [4096, 4096], P('row', 'col'), may hold values from 0 to 0.45
Outputs:
- substrate_section: float32 [4096, 4096], P('row', 'col')
- activator_section: float32 [4096, 4096], P('row', 'col')
All inputs are finite; a program needn't handle non-finite values.
Results may differ from a plain program's by a relative error of at most 0.00023.
Values sent between devices are 32-bit elements; how exact they have to be, the bound alone decides.
A program may use at most 64 MiB of HBM per device.

v0:
```python
import math

import jax
import jax.numpy as jnp
from jax import lax
from jax.sharding import Mesh
from jax.sharding import PartitionSpec as P

ROW = ("row_0", "row_1", "row_2")


FEED_RATE = 0.037
KILL_RATE = 0.06
TIME_STEP = 8.0
SUBSTRATE_DIFFUSION = 4e-07
ACTIVATOR_DIFFUSION = 2e-07


def split_up(shard, dim, size):
    before, after = (shard.shape[:dim], shard.shape[dim + 1 :])
    return jnp.moveaxis(shard.reshape(*before, size, -1, *after), dim, 0)


def in_order(pieces, dim):
    pieces = jnp.moveaxis(pieces, 0, dim)
    shape = pieces.shape
    return pieces.reshape(*shape[:dim], shape[dim] * shape[dim + 1], *shape[dim + 2 :])


def moved_by_axis(pieces, axes, turns):
    shape = [lax.axis_size(a) for a in axes]
    pieces = pieces.reshape(*shape, *pieces.shape[1:])
    for k in turns:
        pieces = lax.all_to_all(pieces, axes[k], split_axis=k, concat_axis=k, tiled=True)
    return pieces.reshape(-1, *pieces.shape[len(axes) :])


def exchange_by_chip(shard, groups, turns, split_dim, concat_dim):
    size = lax.axis_size(groups[0]) * lax.axis_size(groups[1])
    pieces = split_up(shard, split_dim, size)
    return in_order(moved_by_axis(pieces, groups, turns), concat_dim)


def rotation(left_index, right_index, period, direction):
    phase_index = left_index * right_index % period
    angles = phase_index.astype(jnp.float32) * (2.0 * math.pi / period)
    return (jnp.cos(angles), direction * jnp.sin(angles))


def complex_matrix(size_count, direction):
    indices = jnp.arange(size_count, dtype=jnp.int32)
    cosine_part, sine_part = rotation(indices[:, None], indices[None, :], size_count, direction)
    return jnp.stack([jnp.stack([cosine_part, -sine_part]), jnp.stack([sine_part, cosine_part])])


def transform_last(values, direction):
    part_count, species, middle, length = values.shape
    leading = 64
    second = length // leading
    shaped = values.reshape(part_count, species, middle, leading, second)
    first_matrix = complex_matrix(leading, direction)
    first_pass = jnp.einsum(
        "pqka,qsmab->psmkb", first_matrix, shaped, precision=lax.Precision.HIGHEST
    )
    cosine_part, sine_part = rotation(
        jnp.arange(leading, dtype=jnp.int32)[:, None],
        jnp.arange(second, dtype=jnp.int32)[None, :],
        length,
        direction,
    )
    turned = jnp.stack(
        [
            first_pass[0] * cosine_part - first_pass[1] * sine_part,
            first_pass[0] * sine_part + first_pass[1] * cosine_part,
        ]
    )
    second_matrix = complex_matrix(second, direction)
    second_pass = jnp.einsum(
        "pqkb,qsmjb->psmkj", second_matrix, turned, precision=lax.Precision.HIGHEST
    )
    return second_pass.reshape(part_count, species, middle, length)


def signed_squares(wave_index, total):
    signed = jnp.where(2 * wave_index < total, wave_index, wave_index - total).astype(jnp.float32)
    angular = 2.0 * math.pi * signed
    return angular * angular


def section_factors(row_wave, col_wave, total_rows, total_cols):
    wave_number = signed_squares(row_wave, total_rows) + signed_squares(col_wave, total_cols)
    normalize = 1.0 / (total_rows * total_cols)
    growths = []
    forcings = []
    for diffusion, decay_rate in (
        (SUBSTRATE_DIFFUSION, FEED_RATE),
        (ACTIVATOR_DIFFUSION, FEED_RATE + KILL_RATE),
    ):
        linear = -diffusion * wave_number - decay_rate
        exponent = linear * (0.5 * TIME_STEP)
        growths.append(jnp.exp(exponent) * normalize)
        forcings.append(jnp.expm1(exponent) / linear * normalize)
    return (jnp.stack(growths), jnp.stack(forcings))


def advance(spectra, growth, forcing):
    real_part = spectra[0]
    imag_part = spectra[1]
    return jnp.stack(
        [growth * real_part + forcing * imag_part, growth * imag_part - forcing * real_part]
    )


def col_forward(values):
    return lax.all_to_all(values, "col", split_axis=2, concat_axis=3, tiled=True)


def col_backward(values):
    return lax.all_to_all(values, "col", split_axis=3, concat_axis=2, tiled=True)


def row_forward(values):
    return lax.all_to_all(values, ROW, split_axis=2, concat_axis=3, tiled=True)


def row_backward(values):
    return exchange_by_chip(values, (("row_0", "row_1"), "row_2"), (1, 0), 3, 2)


def on_device(substrate, activator):
    row_count, col_count = substrate.shape
    total_rows = row_count * lax.axis_size(ROW)
    total_cols = col_count * lax.axis_size("col")
    row_index = lax.axis_index(ROW)
    col_index = lax.axis_index("col")
    reaction = substrate * activator * activator
    fields = jnp.stack(
        [jnp.stack([substrate, activator]), jnp.stack([FEED_RATE - reaction, reaction])]
    )
    spectra = transform_last(col_forward(fields), -1)
    spectra = row_forward(col_forward(jnp.swapaxes(spectra, 2, 3)))
    spectra = transform_last(spectra, -1)
    local_cols = col_count // lax.axis_size(ROW)
    col_wave = (
        col_count * col_index
        + local_cols * row_index
        + jnp.arange(local_cols, dtype=jnp.int32)[:, None]
    )
    row_wave = jnp.arange(total_rows, dtype=jnp.int32)[None, :]
    growth, forcing = section_factors(row_wave, col_wave, total_rows, total_cols)
    spectra = transform_last(advance(spectra, growth, forcing), 1)
    spectra = col_backward(row_backward(spectra))
    spectra = jnp.swapaxes(spectra, 2, 3)
    spectra = transform_last(spectra, 1)
    fields = lax.all_to_all(spectra[:1], "col", split_axis=3, concat_axis=2, tiled=True)
    return (fields[0, 0], fields[0, 1])


def solution(mesh):
    split = Mesh(
        mesh.devices.reshape(8, 2, 2, mesh.shape["col"]), ("row_0", "row_1", "row_2", "col")
    )
    placed = (P(ROW, "col"), P(ROW, "col"))
    return jax.shard_map(
        on_device,
        mesh=split,
        in_specs=placed,
        out_specs=(P(ROW, "col"), P(ROW, "col")),
        check_vma=False,
    )
```

profile of v0, /device:TPU:1, one launch (start us, length us, event | category | flops | bytes accessed | tf_op | source)
XLA Modules:
  0.0 238.1 jit_solution(18441862085176898476)
XLA Ops:
  0.6 1.0 stack.54
  1.6 1.0 stack.53
  2.6 1.0 subtract_bitcast_fusion
  3.9 0.5 maximum_bitcast_fusion.10
  4.4 1.0 pad_maximum_fusion.1
  5.4 10.2 %all-to-all-start = ((f32[2,2,128,256]{3,1,0,2:T(2,128)}), f32[2,2,128,256]{3,1,0,2:T(2,128)S(1)}, u32[]{:S(2)}, u32[]{:S(2)}) async-start(f32[2,2,128,256]{3,1,0,2:T(2,128)} %pad_maximum_fusion.1), calls=%async_computation | async-start | bytes 1048576 | tf_op jit(solution)/shard_map/all_to_all | solution.py:115
  16.2 16.6 %all-to-all-done = f32[2,2,128,256]{3,1,0,2:T(2,128)S(1)} async-done(((f32[2,2,128,256]{3,1,0,2:T(2,128)}), f32[2,2,128,256]{3,1,0,2:T(2,128)S(1)}, u32[]{:S(2)}, u32[]{:S(2)}) %all-to-all-start) | async-done | bytes 524320 | tf_op jit(solution)/shard_map/all_to_all | solution.py:115
  32.8 0.3 copy.128
  33.1 0.2 reshape.419
  33.3 1.8 convolution_bitcast_fusion.7
  35.3 1.8 convolution_bitcast_fusion.6
  37.1 0.3 copy.65
  37.5 0.4 reshape.420
  37.8 8.2 %copy.66 = f32[2,2,4096,8]{3,1,0,2:T(2,128)} copy(f32[2,2,4096,8]{2,3,1,0:T(8,128)S(1)} %bitcast.164) | data formatting | bytes 1048576 | tf_op jit(solution)/shard_map/transpose | solution.py:141
  46.0 14.9 %reshape.444 = f32[16,1,8192]{2,1,0:T(1,128)S(1)} reshape(f32[4096,2,2,8]{3,2,1,0:T(2,128)} %bitcast.160) | data formatting | bytes 1048576
  61.0 21.9 %all_to_all.94 = f32[16,1,8192]{2,1,0:T(1,128)S(1)} all-to-all(f32[16,1,8192]{2,1,0:T(1,128)S(1)} %reshape.444), channel_id=1, replica_groups=mesh['row_0'=8,'row_1'=2,'row_2'=2,'col'=16] {'col'}, dimensions={0} | all-to-all | bytes 1048576 | tf_op jit(solution)/shard_map/all_to_all | solution.py:115
  82.8 0.5 broadcast.663
  83.3 1.9 reduce
  85.2 14.7 %reshape.445 = f32[4096,2,2,8]{3,2,1,0:T(2,128)} reshape(f32[16,8192]{1,0:T(8,128)S(1)} %reduce) | data formatting | bytes 1048576
  100.0 9.5 %copy.67 = f32[2,2,4096,8]{2,3,1,0:T(8,128)S(1)} copy(f32[2,2,4096,8]{3,1,0,2:T(2,128)} %bitcast.161) | data formatting | bytes 1048576 | tf_op jit(solution)/shard_map/all_to_all | solution.py:115
  109.5 1.0 copy.68
  110.5 13.2 %all-to-all-start.2 = ((f32[2,2,256,128]{3,1,0,2:T(2,128)}), f32[2,2,256,128]{3,1,0,2:T(2,128)S(1)}, u32[]{:S(2)}, u32[]{:S(2)}) async-start(f32[2,2,256,128]{3,1,0,2:T(2,128)} %copy.68), calls=%async_computation.2 | async-start | bytes 1048576 | tf_op jit(solution)/shard_map/all_to_all | solution.py:123
  123.9 0.3 fusion.18
  124.3 16.0 %all-to-all-done.2 = f32[2,2,256,128]{3,1,0,2:T(2,128)S(1)} async-done(((f32[2,2,256,128]{3,1,0,2:T(2,128)}), f32[2,2,256,128]{3,1,0,2:T(2,128)S(1)}, u32[]{:S(2)}, u32[]{:S(2)}) %all-to-all-start.2) | async-done | bytes 524320 | tf_op jit(solution)/shard_map/all_to_all | solution.py:123
  140.4 0.2 reshape.421
  140.6 1.8 convolution_bitcast_fusion.5
  142.6 1.8 convolution_bitcast_fusion.4
  144.4 0.3 multiply_add_fusion.2
  144.7 1.0 convolution_bitcast_fusion.3
  145.9 1.8 convolution_bitcast_fusion.2
  147.7 0.3 copy.74
  148.1 0.2 reshape_reshape.3
  148.3 5.1 %all_to_all.95 = f32[16,2,2,2,8,128]{5,0,4,3,2,1:T(8,128)S(1)} all-to-all(f32[16,2,2,2,8,128]{5,0,4,3,2,1:T(8,128)S(1)} %copy.75), channel_id=1, replica_groups=mesh['row_0'=8,'row_1'=2,'row_2'=2,'col'=16] {'row_2'}, dimensions={1} | all-to-all | bytes 1048576 | tf_op jit(solution)/shard_map/all_to_all | solution.py:34
  153.4 0.4 copy.76
  153.9 18.7 %all_to_all.96 = f32[16,2,2,2,8,128]{5,1,4,3,2,0:T(2,128)S(1)} all-to-all(f32[16,2,2,2,8,128]{5,1,4,3,2,0:T(2,128)S(1)} %copy.76), channel_id=1, replica_groups=mesh['row_0'=8,'row_1'=2,'row_2'=2,'col'=16] {'row_0','row_1'}, dimensions={0} | all-to-all | bytes 1048576 | tf_op jit(solution)/shard_map/all_to_all | solution.py:34
  172.6 0.3 copy.78
  172.9 17.8 %all_to_all.97 = f32[2,2,256,128]{2,1,0,3:T(2,128)S(1)} all-to-all(f32[2,2,256,128]{2,1,0,3:T(2,128)S(1)} %copy.78), channel_id=1, replica_groups=mesh['row_0'=8,'row_1'=2,'row_2'=2,'col'=16] {'col'}, dimensions={3} | all-to-all | bytes 1048576 | tf_op jit(solution)/shard_map/all_to_all | solution.py:119
  190.8 0.4 reshape.425
  191.2 1.8 convolution_bitcast_fusion.1
  193.1 0.2 multiply_subtract_fusion
  193.2 1.8 convolution_bitcast_fusion
  195.1 4.8 %copy.117 = f32[1,2,8,64,64]{2,1,4,3,0:T(2,128)} copy(f32[1,2,8,64,64]{3,4,0,2,1:T(8,128)S(1)} %slice.76) | data formatting | bytes 524288 | tf_op jit(solution)/shard_map/slice | solution.py:155
  199.9 8.3 %reshape.446 = f32[16,1,4096]{2,1,0:T(1,128)S(1)} reshape(f32[4096,1,2,8]{3,2,1,0:T(2,128)} %bitcast.162) | data formatting | bytes 524288
  208.2 15.2 %all_to_all.98 = f32[16,1,4096]{2,1,0:T(1,128)S(1)} all-to-all(f32[16,1,4096]{2,1,0:T(1,128)S(1)} %reshape.446), channel_id=1, replica_groups=mesh['row_0'=8,'row_1'=2,'row_2'=2,'col'=16] {'col'}, dimensions={0} | all-to-all | bytes 524288 | tf_op jit(solution)/shard_map/all_to_all | solution.py:155
  223.4 1.3 reduce.1
  224.6 7.7 %reshape.447 = f32[4096,1,2,8]{3,2,1,0:T(2,128)} reshape(f32[16,4096]{1,0:T(8,128)S(1)} %reduce.1) | data formatting | bytes 524288
  232.3 5.1 %copy.84 = f32[1,2,16,8,256]{4,3,2,1,0:T(8,128)S(1)} copy(f32[1,2,16,8,256]{3,1,4,2,0:T(2,128)} %bitcast.163) | data formatting | bytes 524288 | tf_op jit(solution)/shard_map/all_to_all | solution.py:155
  237.4 0.7 slice_bitcast_fusion
  (19 shorter events, 1.8 us)
Async XLA Ops:
  5.4 27.4 %all-to-all-start = ((f32[2,2,128,256]{3,1,0,2:T(2,128)}), f32[2,2,128,256]{3,1,0,2:T(2,128)S(1)}, u32[]{:S(2)}, u32[]{:S(2)}) async-start(f32[2,2,128,256]{3,1,0,2:T(2,128)} %pad_maximum_fusion.1), calls=%async_computation | async-start | bytes 1048576 | tf_op jit(solution)/shard_map/all_to_all | solution.py:115
  110.5 29.8 %all-to-all-start.2 = ((f32[2,2,256,128]{3,1,0,2:T(2,128)}), f32[2,2,256,128]{3,1,0,2:T(2,128)S(1)}, u32[]{:S(2)}, u32[]{:S(2)}) async-start(f32[2,2,256,128]{3,1,0,2:T(2,128)} %copy.68), calls=%async_computation.2 | async-start | bytes 1048576 | tf_op jit(solution)/shard_map/all_to_all | solution.py:123
where the time goes:
time: 241 us; the launch traced here: 238 us
  local copies, waits for them, and re-layouts  81 us (34%)
  blocking collectives  78.7 us (33%)
  waiting for transfers between devices  32.6 us (14%)
  starting transfers between devices  23.4 us (10%)
  matrix products  13.7 us (6%)
  other arithmetic  7.65 us (3%)
    unnamed x4, local copies, waits for them, and re-layouts  45.6 us
    all_to_all x2, blocking collectives, moved_by_axis(): lax.all_to_all(pieces, axes[k], split_axis=k, concat_axis=k, tiled=True)  23.8 us
    all_to_all x1, blocking collectives, col_forward(): lax.all_to_all(values, 'col', split_axis=2, concat_axis=3, tiled=True)  21.9 us
    all_to_all x1, blocking collectives, col_backward(): lax.all_to_all(values, 'col', split_axis=3, concat_axis=2, tiled=True)  17.8 us
    all_to_all x1, waiting for transfers between devices, col_forward(): lax.all_to_all(values, 'col', split_axis=2, concat_axis=3, tiled=True)  16.6 us
    all_to_all x1, waiting for transfers between devices, row_forward(): return lax.all_to_all(values, ROW, split_axis=2, concat_axis=3, tiled=True)  16 us
    all_to_all x1, blocking collectives, on_device(): lax.all_to_all(spectra[:1], 'col', split_axis=3, concat_axis=2, tiled=True)  15.2 us
    all_to_all x1, starting transfers between devices, row_forward(): return lax.all_to_all(values, ROW, split_axis=2, concat_axis=3, tiled=True)  13.2 us
  transfers between devices with their start and end apart: 2, of which 2 were waited for; matrix products, arithmetic and copies ran while one was open for 0% of the time, Pallas kernels for 0%

commit v1 on v0

v1 whole, which is shorter than its diff:
```python
import math

import jax
import jax.numpy as jnp
import numpy as np
from jax import lax
from jax.experimental import pallas as pl
from jax.experimental.pallas import tpu as pltpu
from jax.sharding import PartitionSpec as P

FEED_RATE = 0.037
KILL_RATE = 0.06
HALF_STEP = 4.0
SUBSTRATE = (4e-07, FEED_RATE)
ACTIVATOR = (2e-07, FEED_RATE + KILL_RATE)
TOTAL = 4096
COLS = 16
ROWS = 32
WIDE = 256
LANES = 128
F32 = jnp.float32
BF16 = jnp.bfloat16


def c_add(a, b):
    im = a[1] if b[1] is None else (b[1] if a[1] is None else a[1] + b[1])
    return (a[0] + b[0], im)


def c_sub(a, b):
    im = a[1] if b[1] is None else (-b[1] if a[1] is None else a[1] - b[1])
    return (a[0] - b[0], im)


def c_conj(a):
    return (a[0], None if a[1] is None else -a[1])


def c_turn(a, numerator, denominator):
    numerator %= denominator
    if numerator == 0:
        return a
    if 4 * numerator == denominator:
        return (jnp.zeros_like(a[0]) if a[1] is None else -a[1], a[0])
    if 4 * numerator == 3 * denominator:
        return (jnp.zeros_like(a[0]) if a[1] is None else a[1], -a[0])
    cosine = math.cos(2.0 * math.pi * numerator / denominator)
    sine = math.sin(2.0 * math.pi * numerator / denominator)
    if a[1] is None:
        return (a[0] * cosine, a[0] * sine)
    return (a[0] * cosine - a[1] * sine, a[0] * sine + a[1] * cosine)


def real_forward(values):
    size = len(values)
    if size == 2:
        return [(values[0] + values[1], None), (values[0] - values[1], None)]
    even, odd = real_forward(values[::2]), real_forward(values[1::2])
    return join_halves(even, odd, size)


def join_halves(even, odd, size, first=0):
    half = size // 2
    out = [None] * (half + 1)
    for k in range(first, half // 2 + 1):
        turned = c_turn(odd[k], -k, size)
        out[k] = c_add(even[k], turned)
        if half - k != k:
            out[half - k] = c_conj(c_sub(even[k], turned))
    return out


def split_halves(spectrum, size, first=0):
    half = size // 2
    even, odd = [None] * (half // 2 + 1), [None] * (half // 2 + 1)
    for k in range(first, half // 2 + 1):
        if k == 0:
            even[k] = (spectrum[0][0] + spectrum[half][0], None)
            odd[k] = (spectrum[0][0] - spectrum[half][0], None)
        elif 2 * k == half:
            even[k] = (2.0 * spectrum[k][0], None)
            odd[k] = (-2.0 * spectrum[k][1], None)
        else:
            other = c_conj(spectrum[half - k])
            even[k] = c_add(spectrum[k], other)
            odd[k] = c_turn(c_sub(spectrum[k], other), k, size)
    return even, odd


def real_backward(spectrum):
    size = 2 * (len(spectrum) - 1)
    if size == 2:
        a, b = spectrum[0][0], spectrum[1][0]
        return [a + b, a - b]
    even, odd = split_halves(spectrum, size)
    even, odd = real_backward(even), real_backward(odd)
    return [x for pair in zip(even, odd) for x in pair]


def roll_rows(tile, shift):
    return pltpu.roll(tile, shift, 0)


def sublane():
    return lax.broadcasted_iota(jnp.int32, (8, LANES), 0)


def part_sign():
    return jnp.where(sublane() < 4, 1.0, -1.0).astype(F32)


def tile_turn(tile, sign, cosine, sine):
    return tile * cosine - (sign * sine) * roll_rows(tile, 4)


def tile_fft(tiles, sign, direction):
    size = len(tiles)
    if size == 1:
        return tiles
    even, odd = tile_fft(tiles[::2], sign, direction), tile_fft(tiles[1::2], sign, direction)
    low, high = [], []
    for k in range(size // 2):
        turned = odd[k]
        if 4 * k == size:
            turned = (-direction * sign) * roll_rows(turned, 4)
        elif k:
            angle = direction * 2.0 * math.pi * k / size
            turned = tile_turn(turned, sign, math.cos(angle), math.sin(angle))
        low.append(even[k] + turned)
        high.append(even[k] - turned)
    return low + high


def dot3(values, high, low, dims):
    dot = lambda a, b: lax.dot_general(a, b, (dims, ((), ())), preferred_element_type=F32)
    top = values.astype(BF16)
    rest = (values - top.astype(F32)).astype(BF16)
    return dot(top, high) + (dot(rest, high) + dot(top, low))


FORWARD = ((1,), (0,))
BACKWARD = ((1,), (1,))


def forward_columns(values, turn_cos, turn_sin, weights):
    even, odd = real_forward(values[::2]), real_forward(values[1::2])
    spectrum = join_halves(even, odd, COLS, 1)
    rows = [jnp.concatenate([even[0][0], odd[0][0]], axis=1)]
    for k in range(1, COLS // 2):
        re, im = spectrum[k]
        cosine, sine = turn_cos[k : k + 1, :], turn_sin[k : k + 1, :]
        rows.append(jnp.concatenate([re * cosine + im * sine, im * cosine - re * sine], axis=1))
    stacked = jnp.concatenate(rows, axis=0)
    out = dot3(stacked, weights[0], weights[1], FORWARD)
    first = dot3(stacked[:16], weights[2], weights[3], FORWARD)
    blocks = []
    for slot in range(COLS // 2):
        row = first[:8] if slot == 0 else out[8 * slot : 8 * slot + 8]
        blocks += [row[:, :WIDE], row[:, WIDE:]]
    return blocks


def backward_columns(blocks, turn_cos, turn_sin, weights):
    stacked = jnp.concatenate(
        [jnp.concatenate([blocks[2 * s], blocks[2 * s + 1]], axis=1) for s in range(COLS // 2)],
        axis=0,
    )
    out = dot3(stacked, weights[0], weights[1], BACKWARD)
    first = dot3(stacked[:16], weights[2], weights[3], BACKWARD)
    spectrum = [None] * (COLS // 2)
    for k in range(1, COLS // 2):
        row = out[8 * k : 8 * k + 8]
        re, im = row[:, :WIDE], row[:, WIDE:]
        cosine, sine = turn_cos[k : k + 1, :], turn_sin[k : k + 1, :]
        spectrum[k] = (re * cosine - im * sine, im * cosine + re * sine)
    even, odd = split_halves(spectrum + [None], COLS, 1)
    even[0], odd[0] = (first[:8, :WIDE], None), (first[:8, WIDE:], None)
    even, odd = real_backward(even), real_backward(odd)
    return [x for pair in zip(even, odd) for x in pair]


def squared_wave(index):
    signed = jnp.where(2 * index < TOTAL, index, index - TOTAL).astype(F32)
    angular = (2.0 * math.pi) * signed
    return angular * angular


def growth_forcing(wave_number, diffusion, decay_rate):
    linear = -diffusion * wave_number - decay_rate
    growth = jnp.exp(HALF_STEP * linear)
    return growth, (growth - 1.0) / linear


def factors(step, row, col):
    column = sublane() % 4
    slot, half = col // 2, col % 2
    within = LANES * half + 4 * row + column
    q = jnp.where(slot == 0, 8 * within, slot + COLS * within)
    p = step + ROWS * lax.broadcasted_iota(jnp.int32, (8, LANES), 1)
    row_wave = squared_wave(p)
    wave_number = row_wave + squared_wave(q)
    norm = 1.0 / (TOTAL * TOTAL)
    paired = jnp.where(q == 0, 1.0, jnp.where(slot == 0, 2.0, 1.0)).astype(F32)
    scale = paired * norm
    growth_s, forcing_s = growth_forcing(wave_number, *SUBSTRATE)
    growth_a, forcing_a = growth_forcing(wave_number, *ACTIVATOR)
    last = row_wave + (2.0 * math.pi * (TOTAL // 2)) ** 2
    first = column == 0
    growth_e, forcing_e = growth_forcing(
        last,
        jnp.where(first, SUBSTRATE[0], ACTIVATOR[0]).astype(F32),
        jnp.where(first, SUBSTRATE[1], ACTIVATOR[1]).astype(F32),
    )
    signed = jnp.where(first, -norm, norm).astype(F32)
    return (
        growth_s * scale,
        forcing_s * scale,
        growth_a * scale,
        forcing_a * scale,
        growth_e * norm,
        forcing_e * signed,
    )


def advance(substrate, activator, reaction, tables):
    growth_s, forcing_s, growth_a, forcing_a, growth_e, forcing_e = tables
    first = sublane() % 4 == 0
    both = jnp.where(first, substrate, roll_rows(activator, 1))
    source = jnp.where(first, reaction, roll_rows(reaction, 1))
    return (
        growth_s * substrate - forcing_s * reaction,
        growth_a * activator + forcing_a * reaction,
        growth_e * both + forcing_e * source,
    )


def constants():
    def split(matrix):
        high = matrix.astype(np.float32).astype(BF16)
        return high, (matrix - high.astype(np.float64)).astype(np.float32).astype(BF16)

    def interleave(re, im):
        size = re.shape[0]
        return np.stack([re.reshape(size, -1, 4), im.reshape(size, -1, 4)], axis=2).reshape(size, -1)

    j = np.arange(WIDE)
    angle = 2.0 * np.pi * (np.outer(j, j) % WIDE) / WIDE
    cos, sin = np.cos(angle), np.sin(angle)
    pair = interleave(np.concatenate([cos, sin]), np.concatenate([-sin, cos]))
    long = np.arange(2 * WIDE)
    angle = 2.0 * np.pi * (np.outer(long, j) % (2 * WIDE)) / (2 * WIDE)
    cos, sin = np.cos(angle), -np.sin(angle)
    sin[:, 0] = 1.0 - 2.0 * (long % 2)
    single = interleave(cos, sin)
    wide = np.stack([*split(pair), *split(single)])
    i = np.arange(LANES)
    angle = 2.0 * np.pi * (np.outer(i, i) % LANES) / LANES
    tall = np.stack(split(np.concatenate([np.cos(angle), np.sin(angle)], axis=1)))

    def turns(count, size):
        angle = 2.0 * np.pi * np.outer(np.arange(count), np.arange(size)) / TOTAL
        return np.stack([np.cos(angle), np.sin(angle)]).astype(np.float32)

    return wide, tall, turns(COLS // 2, WIDE), turns(ROWS, LANES)


SEND1, SEND2, SEND3, SEND4, SEND5, SEND6 = 0, 1, 4, 7, 9, 11


def kernel(
    u_hbm, v_hbm, wide_hbm, tall_hbm, turn1_hbm, turn2_hbm, s_out, a_out,
    fields, wide, tall, turn1, turn2, tables,
    got1, put2, got2, put3, got3, tiles, products, filtered, extra,
    put4, got4, put5, got5, put6, local_sem, send_sem, recv_sem,
):
    row, col = lax.axis_index("row"), lax.axis_index("col")
    mesh_id = pl.DeviceIdType.MESH

    loads = [
        pltpu.make_async_copy(src, dst, local_sem.at[n])
        for n, (src, dst) in enumerate(
            [
                (u_hbm, fields.at[0]),
                (v_hbm, fields.at[1]),
                (wide_hbm, wide),
                (tall_hbm, tall),
                (turn1_hbm, turn1),
                (turn2_hbm, turn2),
            ]
        )
    ]
    for load in loads:
        load.start()

    barrier = pltpu.get_barrier_semaphore()

    def greet(axis, me, size):
        def body(k, carry):
            pl.semaphore_signal(
                barrier, inc=1, device_id={axis: lax.rem(me + k, size)}, device_id_type=mesh_id
            )
            return carry

        lax.fori_loop(1, size, body, 0)

    greet("col", col, COLS)
    greet("row", row, ROWS)

    def send(axis, me, size, source, target, sem):
        def body(k, carry):
            peer = lax.rem(me + k, size)
            pltpu.make_async_remote_copy(
                src_ref=source(peer),
                dst_ref=target(me),
                send_sem=send_sem.at[sem],
                recv_sem=recv_sem.at[sem],
                device_id={axis: peer},
                device_id_type=mesh_id,
            ).start()
            return carry

        lax.fori_loop(1, size, body, 0)

    def whole(axis, me, size, block, sem):
        return pltpu.make_async_remote_copy(
            src_ref=block,
            dst_ref=block,
            send_sem=send_sem.at[sem],
            recv_sem=recv_sem.at[sem],
            device_id={axis: lax.rem(me + 1, size)},
            device_id_type=mesh_id,
        )

    pending = []

    def arrived(axis, me, size, block, sem):
        whole(axis, me, size, block, sem).wait_recv()

    def fill(step, carry):
        for n, table in enumerate(factors(step, row, col)):
            tables[n, step] = table
        return carry

    lax.fori_loop(0, ROWS, fill, 0)

    loads[0].wait()
    loads[1].wait()
    pl.semaphore_wait(barrier, COLS - 1 + ROWS - 1)

    send("col", col, COLS, lambda c: fields.at[:, c], lambda c: got1.at[c], SEND1)
    pending.append(("col", col, COLS, got1.at[pl.ds(0, COLS - 1)], SEND1))
    got1[col] = fields[:, col]
    for load in loads[2:]:
        load.wait()
    arrived("col", col, COLS, got1.at[pl.ds(0, COLS - 1)], SEND1)

    for n in range(3):
        if n < 2:
            values = [got1[c, n] for c in range(COLS)]
        else:
            values = [got1[c, 0] * got1[c, 1] * got1[c, 1] for c in range(COLS)]
        weights = [wide.at[k][...] for k in range(4)]
        blocks = forward_columns(values, turn1[0], turn1[1], weights)
        for c in range(COLS):
            put2[n, c] = blocks[c]
        send("col", col, COLS, lambda c: put2.at[n, c], lambda c: got2.at[n, c], SEND2 + n)
        pending.append(("col", col, COLS, put2.at[n, pl.ds(0, COLS - 1)], SEND2 + n))
        got2[n, col] = put2[n, col]

    for n in range(3):
        arrived("col", col, COLS, got2.at[n, pl.ds(0, COLS - 1)], SEND2 + n)
        block = got2[n].reshape(COLS * 8, WIDE)
        put3[n] = block.T.reshape(ROWS, 8, LANES)
        send("row", row, ROWS, lambda r: put3.at[n, r], lambda r: got3.at[n, r], SEND3 + n)
        pending.append(("row", row, ROWS, put3.at[n, pl.ds(0, ROWS - 1)], SEND3 + n))
        got3[n, row] = put3[n, row]

    sign = part_sign()
    for n in range(3):
        arrived("row", row, ROWS, got3.at[n, pl.ds(0, ROWS - 1)], SEND3 + n)
        spectrum = tile_fft([got3[n, r] for r in range(ROWS)], sign, -1)
        for k in range(ROWS):
            cosine, sine = turn2[0, k : k + 1, :], turn2[1, k : k + 1, :]
            tiles[k] = tile_turn(spectrum[k], sign, cosine, -sine)
        out = dot3(tiles[...].reshape(ROWS * 8, LANES), tall[0], tall[1], FORWARD)
        products[n] = out.reshape(ROWS, 8, 2 * LANES)

    def filter_step(k, carry):
        spectra = []
        for n in range(3):
            both = products[n, k]
            spectra.append(both[:, :LANES] + sign * roll_rows(both[:, LANES:], 4))
        for n, tile in enumerate(advance(*spectra, [tables[m, k] for m in range(6)])):
            filtered[n, k] = tile
        return carry

    lax.fori_loop(0, ROWS, filter_step, 0)

    special = sublane() == jnp.where(row + col == 0, 4, -1)
    for n in (2, 0, 1):
        block = filtered[n].reshape(ROWS * 8, LANES)
        products[n] = dot3(block, tall[0], tall[1], FORWARD).reshape(ROWS, 8, 2 * LANES)
        turned = []
        for k in range(ROWS):
            both = products[n, k]
            tile = both[:, :LANES] - sign * roll_rows(both[:, LANES:], 4)
            cosine, sine = turn2[0, k : k + 1, :], turn2[1, k : k + 1, :]
            turned.append(tile_turn(tile, sign, cosine, sine))
        values = tile_fft(turned, sign, 1)
        for r in range(ROWS):
            if n == 2:
                extra[r] = values[r]
            elif n == 0:
                put4[n, r] = jnp.where(special, extra[r], values[r])
            else:
                put4[n, r] = jnp.where(special, roll_rows(extra[r], 7), values[r])
        if n == 2:
            continue
        send("row", row, ROWS, lambda r: put4.at[n, r], lambda r: got4.at[n, r], SEND4 + n)
        pending.append(("row", row, ROWS, put4.at[n, pl.ds(0, ROWS - 1)], SEND4 + n))
        got4[n, row] = put4[n, row]

    for n in range(2):
        arrived("row", row, ROWS, got4.at[n, pl.ds(0, ROWS - 1)], SEND4 + n)
        block = got4[n].reshape(ROWS * 8, LANES)
        put5[n] = block.T.reshape(COLS, 8, WIDE)
        send("col", col, COLS, lambda c: put5.at[n, c], lambda c: got5.at[n, c], SEND5 + n)
        pending.append(("col", col, COLS, put5.at[n, pl.ds(0, COLS - 1)], SEND5 + n))
        got5[n, col] = put5[n, col]

    _, feed = growth_forcing_at_zero()
    last = []
    for n, out in enumerate((s_out, a_out)):
        arrived("col", col, COLS, got5.at[n, pl.ds(0, COLS - 1)], SEND5 + n)
        weights = [wide.at[k][...] for k in range(4)]
        values = backward_columns([got5[n, c] for c in range(COLS)], turn1[0], turn1[1], weights)
        for c in range(COLS):
            put6[n, c] = values[c] + feed if n == 0 else values[c]
        send("col", col, COLS, lambda c: put6.at[n, c], lambda c: out.at[c], SEND6 + n)
        pending.append(("col", col, COLS, put6.at[n, pl.ds(0, COLS - 1)], SEND6 + n))
        own = pltpu.make_async_copy(put6.at[n, col], out.at[col], local_sem.at[n])
        own.start()
        last.append(own)

    for n, out in enumerate((s_out, a_out)):
        arrived("col", col, COLS, out.at[pl.ds(0, COLS - 1)], SEND6 + n)
        last[n].wait()
    for entry in pending:
        whole(*entry).wait_send()


def growth_forcing_at_zero():
    linear = -FEED_RATE
    return math.exp(HALF_STEP * linear), FEED_RATE * math.expm1(HALF_STEP * linear) / linear


def on_device(substrate, activator):
    wide, tall, turn1, turn2 = constants()
    shape = jax.ShapeDtypeStruct((COLS, 8, WIDE), F32)
    anywhere = pl.BlockSpec(memory_space=pl.ANY)
    vmem = lambda *shape: pltpu.VMEM(shape, F32)
    by_col, by_row = (COLS, 8, WIDE), (ROWS, 8, LANES)
    out = pl.pallas_call(
        kernel,
        name="section",
        out_shape=(shape, shape),
        in_specs=[anywhere] * 6,
        out_specs=(anywhere, anywhere),
        scratch_shapes=[
            vmem(2, *by_col),
            pltpu.VMEM(wide.shape, BF16),
            pltpu.VMEM(tall.shape, BF16),
            vmem(*turn1.shape),
            vmem(*turn2.shape),
            vmem(6, *by_row),
            vmem(COLS, 2, 8, WIDE),
            vmem(3, *by_col),
            vmem(3, *by_col),
            vmem(3, *by_row),
            vmem(3, *by_row),
            vmem(*by_row),
            vmem(3, ROWS, 8, 2 * LANES),
            vmem(3, *by_row),
            vmem(*by_row),
            vmem(2, *by_row),
            vmem(2, *by_row),
            vmem(2, *by_col),
            vmem(2, *by_col),
            vmem(2, *by_col),
            pltpu.SemaphoreType.DMA((6,)),
            pltpu.SemaphoreType.DMA((13,)),
            pltpu.SemaphoreType.DMA((13,)),
        ],
        compiler_params=pltpu.CompilerParams(collective_id=0, has_side_effects=True),
    )(
        substrate.reshape(COLS, 8, WIDE),
        activator.reshape(COLS, 8, WIDE),
        wide,
        tall,
        turn1,
        turn2,
    )
    return tuple(x.reshape(substrate.shape) for x in out)


def solution(mesh):
    spec = P("row", "col")
    return jax.shard_map(
        on_device, mesh=mesh, in_specs=(spec, spec), out_specs=(spec, spec), check_vma=False
    )
```

time: 241 us -> 76.3 us (0.32)
  blocking collectives: 78.7 us -> 0 us
  local copies, waits for them, and re-layouts: 81 us -> 3.14 us
  Pallas kernels: 0 us -> 72 us
  waiting for transfers between devices: 32.6 us -> 0 us
  starting transfers between devices: 23.4 us -> 0 us
  matrix products: 13.7 us -> 0 us
  other arithmetic: 7.65 us -> 0 us
    all_to_all x5 -> x0, blocking collectives: 78.7 us -> none  [the longest x2 23.8 us: moved_by_axis(): lax.all_to_all(pieces, axes[k], split_axis=k, concat_axis=k, tiled=True)]
    pallas_call x0 -> x1, Pallas kernels: none -> 72 us  [on_device(): pl.pallas_call(kernel, name='section', out_shape=(shape, shape), in_specs...]
    unnamed x4 -> x2, local copies, waits for them, and re-layouts: 45.6 us -> 3.14 us
    all_to_all x2 -> x0, waiting for transfers between devices: 32.6 us -> none  [the longest x1 16.6 us: col_forward(): lax.all_to_all(values, 'col', split_axis=2, concat_axis=3, tiled=True)]
    all_to_all x2 -> x0, starting transfers between devices: 23.4 us -> none  [the longest x1 13.2 us: row_forward(): return lax.all_to_all(values, ROW, split_axis=2, concat_axis=3, tiled=True)]
    all_to_all x10 -> x0, local copies, waits for them, and re-layouts: 17.1 us -> none  [the longest x4 11.3 us: col_forward(): lax.all_to_all(values, 'col', split_axis=2, concat_axis=3, tiled=True)]
    dot_general x8 -> x0, matrix products: 13.7 us -> none  [the longest x4 7.28 us: transform_last(): jnp.einsum('pqkb,qsmjb->psmkj', second_matrix, turned, precision=lax.Prec...]
    transpose x3 -> x0, local copies, waits for them, and re-layouts: 8.84 us -> none  [the longest x1 8.18 us: on_device(): spectra = row_forward(col_forward(jnp.swapaxes(spectra, 2, 3)))]
  transfers between devices with their start and end apart: 2 -> 0, of which waited for: 2 -> 0; matrix products, arithmetic and copies ran while one was open for 0% -> 0% of each run, Pallas kernels for 0% -> 0%
where the time goes in v1:
time: 76.3 us; the launch traced here: 75.8 us
  Pallas kernels  72 us (94%)
  local copies, waits for them, and re-layouts  3.14 us (4%)
    pallas_call x1, Pallas kernels, on_device(): pl.pallas_call(kernel, name='section', out_shape=(shape, shape), in_specs...  72 us
    unnamed x2, local copies, waits for them, and re-layouts  3.14 us

profile of v1, /device:TPU:1, one launch (start us, length us, event | category | flops | bytes accessed | tf_op | source)
XLA Modules:
  0.0 75.8 jit_solution(10164570849116849114)
XLA Ops:
  0.6 72.0 %section.1 = (f32[16,8,256]{2,1,0:T(8,128)}, f32[16,8,256]{2,1,0:T(8,128)}) custom-call(f32[16,8,256]{2,1,0:T(8,128)} %bitcast.4, f32[16,8,256]{2,1,0:T(8,128)} %bitcast.5, bf16[4,512,512]{2,1,0:T(8,128)(2,1)} %constant.8.clone.wide_hbm, bf16[2,128,256]{2,1,0:T(8,128)(2,1)} %constant.9.clone.tall_hbm, f32[2,8,256]{2,1,0:T(8,128)} %constant.10.clone.turn1_hbm, ...), custom_call_target="tpu_custom_call" | custom-call | tf_op jit(solution)/shard_map/section/pallas_call | solution.py:463
  72.6 1.6 %copy.10 = f32[128,256]{1,0:T(8,128)} copy(f32[128,256]{1,0:T(8,128)} %bitcast.7) | data formatting | bytes 262144
  74.2 1.6 %copy.11 = f32[128,256]{1,0:T(8,128)} copy(f32[128,256]{1,0:T(8,128)} %bitcast.6) | data formatting | bytes 262144

commit v2 on v1

--- a/solution.py
+++ b/solution.py
@@ -139,7 +139,6 @@
 
 
 FORWARD = ((1,), (0,))
-BACKWARD = ((1,), (1,))
 
 
 def forward_columns(values, turn_cos, turn_sin, weights):
@@ -165,8 +164,8 @@
         [jnp.concatenate([blocks[2 * s], blocks[2 * s + 1]], axis=1) for s in range(COLS // 2)],
         axis=0,
     )
-    out = dot3(stacked, weights[0], weights[1], BACKWARD)
-    first = dot3(stacked[:16], weights[2], weights[3], BACKWARD)
+    out = dot3(stacked, weights[0], weights[1], FORWARD)
+    first = dot3(stacked[:16], weights[2], weights[3], FORWARD)
     spectrum = [None] * (COLS // 2)
     for k in range(1, COLS // 2):
         row = out[8 * k : 8 * k + 8]
@@ -199,39 +198,15 @@
     p = step + ROWS * lax.broadcasted_iota(jnp.int32, (8, LANES), 1)
     row_wave = squared_wave(p)
     wave_number = row_wave + squared_wave(q)
+    last = row_wave + (2.0 * math.pi * (TOTAL // 2)) ** 2
     norm = 1.0 / (TOTAL * TOTAL)
     paired = jnp.where(q == 0, 1.0, jnp.where(slot == 0, 2.0, 1.0)).astype(F32)
-    scale = paired * norm
-    growth_s, forcing_s = growth_forcing(wave_number, *SUBSTRATE)
-    growth_a, forcing_a = growth_forcing(wave_number, *ACTIVATOR)
-    last = row_wave + (2.0 * math.pi * (TOTAL // 2)) ** 2
-    first = column == 0
-    growth_e, forcing_e = growth_forcing(
-        last,
-        jnp.where(first, SUBSTRATE[0], ACTIVATOR[0]).astype(F32),
-        jnp.where(first, SUBSTRATE[1], ACTIVATOR[1]).astype(F32),
-    )
-    signed = jnp.where(first, -norm, norm).astype(F32)
-    return (
-        growth_s * scale,
-        forcing_s * scale,
-        growth_a * scale,
-        forcing_a * scale,
-        growth_e * norm,
-        forcing_e * signed,
-    )
-
-
-def advance(substrate, activator, reaction, tables):
-    growth_s, forcing_s, growth_a, forcing_a, growth_e, forcing_e = tables
-    first = sublane() % 4 == 0
-    both = jnp.where(first, substrate, roll_rows(activator, 1))
-    source = jnp.where(first, reaction, roll_rows(reaction, 1))
-    return (
-        growth_s * substrate - forcing_s * reaction,
-        growth_a * activator + forcing_a * reaction,
-        growth_e * both + forcing_e * source,
-    )
+    out = []
+    for species, sign in ((SUBSTRATE, -1.0), (ACTIVATOR, 1.0)):
+        for waves, scale in ((wave_number, paired * norm), (last, norm)):
+            growth, forcing = growth_forcing(waves, *species)
+            out += [growth * scale, forcing * (scale * sign)]
+    return out
 
 
 def constants():
@@ -264,13 +239,14 @@
     return wide, tall, turns(COLS // 2, WIDE), turns(ROWS, LANES)
 
 
-SEND1, SEND2, SEND3, SEND4, SEND5, SEND6 = 0, 1, 4, 7, 9, 11
+SEND1, SEND2, SEND3, SEND4, SEND5, SEND6 = 0, 2, 5, 8, 10, 12
+U, R, V = 0, 1, 2
 
 
 def kernel(
     u_hbm, v_hbm, wide_hbm, tall_hbm, turn1_hbm, turn2_hbm, s_out, a_out,
-    fields, wide, tall, turn1, turn2, tables,
-    got1, put2, got2, put3, got3, tiles, products, filtered, extra,
+    fields, wide, tall, turn1, turn2, tables, back,
+    got1, put2, got2, put3, got3, tiles, spectra, pair, products,
     put4, got4, put5, got5, put6, local_sem, send_sem, recv_sem,
 ):
     row, col = lax.axis_index("row"), lax.axis_index("col")
@@ -303,38 +279,43 @@
 
         lax.fori_loop(1, size, body, 0)
 
+    pending = []
+
+    def piece(axis, peer, source, target, sem):
+        return pltpu.make_async_remote_copy(
+            src_ref=source,
+            dst_ref=target,
+            send_sem=send_sem.at[sem],
+            recv_sem=recv_sem.at[sem],
+            device_id={axis: peer},
+            device_id_type=mesh_id,
+        )
+
+    def send(axis, source, target, sem):
+        me, size = (col, COLS) if axis == "col" else (row, ROWS)
+
+        def body(k, carry):
+            peer = lax.rem(me + k, size)
+            piece(axis, peer, source.at[peer], target.at[me], sem).start()
+            return carry
+
+        lax.fori_loop(1, size, body, 0)
+        pending.append((axis, source, sem))
+
+    def whole(axis, block, sem):
+        me, size = (col, COLS) if axis == "col" else (row, ROWS)
+        block = block.at[pl.ds(0, size - 1)]
+        return piece(axis, lax.rem(me + 1, size), block, block, sem)
+
     greet("col", col, COLS)
     greet("row", row, ROWS)
-
-    def send(axis, me, size, source, target, sem):
-        def body(k, carry):
-            peer = lax.rem(me + k, size)
-            pltpu.make_async_remote_copy(
-                src_ref=source(peer),
-                dst_ref=target(me),
-                send_sem=send_sem.at[sem],
-                recv_sem=recv_sem.at[sem],
-                device_id={axis: peer},
-                device_id_type=mesh_id,
-            ).start()
-            return carry
-
-        lax.fori_loop(1, size, body, 0)
-
-    def whole(axis, me, size, block, sem):
-        return pltpu.make_async_remote_copy(
-            src_ref=block,
-            dst_ref=block,
-            send_sem=send_sem.at[sem],
-            recv_sem=recv_sem.at[sem],
-            device_id={axis: lax.rem(me + 1, size)},
-            device_id_type=mesh_id,
-        )
-
-    pending = []
-
-    def arrived(axis, me, size, block, sem):
-        whole(axis, me, size, block, sem).wait_recv()
+    loads[0].wait()
+    loads[1].wait()
+    pl.semaphore_wait(barrier, COLS - 1 + ROWS - 1)
+
+    for n in range(2):
+        send("col", fields.at[n], got1.at[n], SEND1 + n)
+        got1[n, col] = fields[n, col]
 
     def fill(step, carry):
         for n, table in enumerate(factors(step, row, col)):
@@ -343,108 +324,98 @@
 
     lax.fori_loop(0, ROWS, fill, 0)
 
-    loads[0].wait()
-    loads[1].wait()
-    pl.semaphore_wait(barrier, COLS - 1 + ROWS - 1)
-
-    send("col", col, COLS, lambda c: fields.at[:, c], lambda c: got1.at[c], SEND1)
-    pending.append(("col", col, COLS, got1.at[pl.ds(0, COLS - 1)], SEND1))
-    got1[col] = fields[:, col]
+    def forward_rows(n, values):
+        blocks = forward_columns(
+            values, turn1[0], turn1[1], [wide.at[k][...] for k in range(4)]
+        )
+        for c in range(COLS):
+            put2[n, c] = blocks[c]
+        send("col", put2.at[n], got2.at[n], SEND2 + n)
+        got2[n, col] = put2[n, col]
+
     for load in loads[2:]:
         load.wait()
-    arrived("col", col, COLS, got1.at[pl.ds(0, COLS - 1)], SEND1)
-
-    for n in range(3):
-        if n < 2:
-            values = [got1[c, n] for c in range(COLS)]
-        else:
-            values = [got1[c, 0] * got1[c, 1] * got1[c, 1] for c in range(COLS)]
-        weights = [wide.at[k][...] for k in range(4)]
-        blocks = forward_columns(values, turn1[0], turn1[1], weights)
-        for c in range(COLS):
-            put2[n, c] = blocks[c]
-        send("col", col, COLS, lambda c: put2.at[n, c], lambda c: got2.at[n, c], SEND2 + n)
-        pending.append(("col", col, COLS, put2.at[n, pl.ds(0, COLS - 1)], SEND2 + n))
-        got2[n, col] = put2[n, col]
-
-    for n in range(3):
-        arrived("col", col, COLS, got2.at[n, pl.ds(0, COLS - 1)], SEND2 + n)
+    whole("col", got1.at[0], SEND1).wait_recv()
+    forward_rows(U, [got1[0, c] for c in range(COLS)])
+    whole("col", got1.at[1], SEND1 + 1).wait_recv()
+    forward_rows(R, [got1[0, c] * got1[1, c] * got1[1, c] for c in range(COLS)])
+    forward_rows(V, [got1[1, c] for c in range(COLS)])
+
+    for n in (U, R, V):
+        whole("col", got2.at[n], SEND2 + n).wait_recv()
         block = got2[n].reshape(COLS * 8, WIDE)
         put3[n] = block.T.reshape(ROWS, 8, LANES)
-        send("row", row, ROWS, lambda r: put3.at[n, r], lambda r: got3.at[n, r], SEND3 + n)
-        pending.append(("row", row, ROWS, put3.at[n, pl.ds(0, ROWS - 1)], SEND3 + n))
+        send("row", put3.at[n], got3.at[n], SEND3 + n)
         got3[n, row] = put3[n, row]
 
     sign = part_sign()
-    for n in range(3):
-        arrived("row", row, ROWS, got3.at[n, pl.ds(0, ROWS - 1)], SEND3 + n)
-        spectrum = tile_fft([got3[n, r] for r in range(ROWS)], sign, -1)
+
+    def forward_down(n):
+        whole("row", got3.at[n], SEND3 + n).wait_recv()
+        values = tile_fft([got3[n, r] for r in range(ROWS)], sign, -1)
         for k in range(ROWS):
             cosine, sine = turn2[0, k : k + 1, :], turn2[1, k : k + 1, :]
-            tiles[k] = tile_turn(spectrum[k], sign, cosine, -sine)
+            tiles[k] = tile_turn(values[k], sign, cosine, -sine)
         out = dot3(tiles[...].reshape(ROWS * 8, LANES), tall[0], tall[1], FORWARD)
-        products[n] = out.reshape(ROWS, 8, 2 * LANES)
-
-    def filter_step(k, carry):
-        spectra = []
-        for n in range(3):
-            both = products[n, k]
-            spectra.append(both[:, :LANES] + sign * roll_rows(both[:, LANES:], 4))
-        for n, tile in enumerate(advance(*spectra, [tables[m, k] for m in range(6)])):
-            filtered[n, k] = tile
-        return carry
-
-    lax.fori_loop(0, ROWS, filter_step, 0)
+        products[pl.ds(0, ROWS)] = out.reshape(ROWS, 8, 2 * LANES)
+        for k in range(ROWS):
+            both = products[k]
+            spectra[n, k] = both[:, :LANES] + sign * roll_rows(both[:, LANES:], 4)
 
     special = sublane() == jnp.where(row + col == 0, 4, -1)
-    for n in (2, 0, 1):
-        block = filtered[n].reshape(ROWS * 8, LANES)
-        products[n] = dot3(block, tall[0], tall[1], FORWARD).reshape(ROWS, 8, 2 * LANES)
-        turned = []
+
+    def backward_down(n, field):
         for k in range(ROWS):
-            both = products[n, k]
-            tile = both[:, :LANES] - sign * roll_rows(both[:, LANES:], 4)
-            cosine, sine = turn2[0, k : k + 1, :], turn2[1, k : k + 1, :]
-            turned.append(tile_turn(tile, sign, cosine, sine))
-        values = tile_fft(turned, sign, 1)
-        for r in range(ROWS):
-            if n == 2:
-                extra[r] = values[r]
-            elif n == 0:
-                put4[n, r] = jnp.where(special, extra[r], values[r])
-            else:
-                put4[n, r] = jnp.where(special, roll_rows(extra[r], 7), values[r])
-        if n == 2:
-            continue
-        send("row", row, ROWS, lambda r: put4.at[n, r], lambda r: got4.at[n, r], SEND4 + n)
-        pending.append(("row", row, ROWS, put4.at[n, pl.ds(0, ROWS - 1)], SEND4 + n))
+            own, source = spectra[field, k], spectra[R, k]
+            for m in range(2):
+                t = 4 * n + 2 * m
+                pair[m * ROWS + k] = tables[t, k] * own + tables[t + 1, k] * source
+        block = pair[...].reshape(2 * ROWS * 8, LANES)
+        products[...] = dot3(block, tall[0], tall[1], FORWARD).reshape(2 * ROWS, 8, 2 * LANES)
+        for m in (1, 0):
+            turned = []
+            for k in range(ROWS):
+                both = products[m * ROWS + k]
+                tile = both[:, :LANES] - sign * roll_rows(both[:, LANES:], 4)
+                cosine, sine = turn2[0, k : k + 1, :], turn2[1, k : k + 1, :]
+                turned.append(tile_turn(tile, sign, cosine, sine))
+            values = tile_fft(turned, sign, 1)
+            for r in range(ROWS):
+                if m == 1:
+                    tiles[r] = values[r]
+                else:
+                    put4[n, r] = jnp.where(special, tiles[r], values[r])
+        send("row", put4.at[n], got4.at[n], SEND4 + n)
         got4[n, row] = put4[n, row]
 
+    forward_down(U)
+    forward_down(R)
+    backward_down(0, U)
+    forward_down(V)
+    backward_down(1, V)
+
+    for k in range(4):
+        back[k] = wide.at[k][...].T
+
     for n in range(2):
-        arrived("row", row, ROWS, got4.at[n, pl.ds(0, ROWS - 1)], SEND4 + n)
+        whole("row", got4.at[n], SEND4 + n).wait_recv()
         block = got4[n].reshape(ROWS * 8, LANES)
         put5[n] = block.T.reshape(COLS, 8, WIDE)
-        send("col", col, COLS, lambda c: put5.at[n, c], lambda c: got5.at[n, c], SEND5 + n)
-        pending.append(("col", col, COLS, put5.at[n, pl.ds(0, COLS - 1)], SEND5 + n))
+        send("col", put5.at[n], got5.at[n], SEND5 + n)
         got5[n, col] = put5[n, col]
 
     _, feed = growth_forcing_at_zero()
-    last = []
     for n, out in enumerate((s_out, a_out)):
-        arrived("col", col, COLS, got5.at[n, pl.ds(0, COLS - 1)], SEND5 + n)
-        weights = [wide.at[k][...] for k in range(4)]
+        whole("col", got5.at[n], SEND5 + n).wait_recv()
+        weights = [back.at[k][...] for k in range(4)]
         values = backward_columns([got5[n, c] for c in range(COLS)], turn1[0], turn1[1], weights)
         for c in range(COLS):
             put6[n, c] = values[c] + feed if n == 0 else values[c]
-        send("col", col, COLS, lambda c: put6.at[n, c], lambda c: out.at[c], SEND6 + n)
-        pending.append(("col", col, COLS, put6.at[n, pl.ds(0, COLS - 1)], SEND6 + n))
-        own = pltpu.make_async_copy(put6.at[n, col], out.at[col], local_sem.at[n])
-        own.start()
-        last.append(own)
+        send("col", put6.at[n], out, SEND6 + n)
+        out[col] = put6[n, col]
 
     for n, out in enumerate((s_out, a_out)):
-        arrived("col", col, COLS, out.at[pl.ds(0, COLS - 1)], SEND6 + n)
-        last[n].wait()
+        whole("col", out, SEND6 + n).wait_recv()
     for entry in pending:
         whole(*entry).wait_send()
 
@@ -456,8 +427,9 @@
 
 def on_device(substrate, activator):
     wide, tall, turn1, turn2 = constants()
-    shape = jax.ShapeDtypeStruct((COLS, 8, WIDE), F32)
-    anywhere = pl.BlockSpec(memory_space=pl.ANY)
+    shape = pltpu.VMEM((COLS, 8, WIDE), F32)
+    held = lambda x: pltpu.with_memory_space_constraint(x, pltpu.HBM)
+    anywhere = pl.BlockSpec(memory_space=pltpu.HBM)
     vmem = lambda *shape: pltpu.VMEM(shape, F32)
     by_col, by_row = (COLS, 8, WIDE), (ROWS, 8, LANES)
     out = pl.pallas_call(
@@ -465,40 +437,43 @@
         name="section",
         out_shape=(shape, shape),
         in_specs=[anywhere] * 6,
-        out_specs=(anywhere, anywhere),
+        out_specs=(pl.BlockSpec(memory_space=pltpu.VMEM),) * 2,
         scratch_shapes=[
             vmem(2, *by_col),
             pltpu.VMEM(wide.shape, BF16),
             pltpu.VMEM(tall.shape, BF16),
             vmem(*turn1.shape),
             vmem(*turn2.shape),
-            vmem(6, *by_row),
-            vmem(COLS, 2, 8, WIDE),
+            vmem(8, *by_row),
+            pltpu.VMEM(wide.shape, BF16),
+            vmem(2, *by_col),
             vmem(3, *by_col),
             vmem(3, *by_col),
             vmem(3, *by_row),
             vmem(3, *by_row),
             vmem(*by_row),
-            vmem(3, ROWS, 8, 2 * LANES),
             vmem(3, *by_row),
-            vmem(*by_row),
+            vmem(2 * ROWS, 8, LANES),
+            vmem(2 * ROWS, 8, 2 * LANES),
             vmem(2, *by_row),
             vmem(2, *by_row),
             vmem(2, *by_col),
             vmem(2, *by_col),
             vmem(2, *by_col),
             pltpu.SemaphoreType.DMA((6,)),
-            pltpu.SemaphoreType.DMA((13,)),
-            pltpu.SemaphoreType.DMA((13,)),
+            pltpu.SemaphoreType.DMA((14,)),
+            pltpu.SemaphoreType.DMA((14,)),
         ],
-        compiler_params=pltpu.CompilerParams(collective_id=0, has_side_effects=True),
+        compiler_params=pltpu.CompilerParams(
+            collective_id=0, has_side_effects=True, vmem_limit_bytes=20 << 20
+        ),
     )(
-        substrate.reshape(COLS, 8, WIDE),
-        activator.reshape(COLS, 8, WIDE),
-        wide,
-        tall,
-        turn1,
-        turn2,
+        held(substrate.reshape(COLS, 8, WIDE)),
+        held(activator.reshape(COLS, 8, WIDE)),
+        held(jnp.asarray(wide)),
+        held(jnp.asarray(tall)),
+        held(jnp.asarray(turn1)),
+        held(jnp.asarray(turn2)),
     )
     return tuple(x.reshape(substrate.shape) for x in out)
 

time: 76.3 us -> 71 us (0.931)
  Pallas kernels: 72 us -> 68.7 us
  local copies, waits for them, and re-layouts: 3.14 us -> 1.31 us
    pallas_call x1, Pallas kernels: 72 us -> 68.7 us  [on_device(): pl.pallas_call(kernel, name='section', out_shape=(shape, shape), in_specs...]
    unnamed x2, local copies, waits for them, and re-layouts: 3.14 us -> 1.31 us
where the time goes in v2:
time: 71 us; the launch traced here: 70.6 us
  Pallas kernels  68.7 us (97%)
  local copies, waits for them, and re-layouts  1.31 us (2%)
    pallas_call x1, Pallas kernels, on_device(): pl.pallas_call(kernel, name='section', out_shape=(shape, shape), in_specs...  68.7 us

profile of v2, /device:TPU:1, one launch (start us, length us, event | category | flops | bytes accessed | tf_op | source)
XLA Modules:
  0.0 70.6 jit_solution(7336381111932401917)
XLA Ops:
  0.6 68.7 %section.1 = (f32[16,8,256]{2,1,0:T(8,128)S(1)}, f32[16,8,256]{2,1,0:T(8,128)S(1)}) custom-call(f32[16,8,256]{2,1,0:T(8,128)} %bitcast.6, f32[16,8,256]{2,1,0:T(8,128)} %bitcast.7, bf16[4,512,512]{2,1,0:T(8,128)(2,1)} %constant.8.clone.wide_hbm, bf16[2,128,256]{2,1,0:T(8,128)(2,1)} %constant.9.clone.tall_hbm, f32[2,8,256]{2,1,0:T(8,128)} %constant.10.clone.turn1_hbm, ...), custom_call_target="tpu_custom_call" | custom-call | tf_op jit(solution)/shard_map/section/pallas_call | solution.py:435
  69.3 0.7 copy.10
  70.0 0.7 copy.11

commit v3 on v2

--- a/solution.py
+++ b/solution.py
@@ -18,6 +18,7 @@
 ROWS = 32
 WIDE = 256
 LANES = 128
+TILES = ROWS // 2
 F32 = jnp.float32
 BF16 = jnp.bfloat16
 
@@ -106,11 +107,15 @@
 
 
 def part_sign():
-    return jnp.where(sublane() < 4, 1.0, -1.0).astype(F32)
-
-
-def tile_turn(tile, sign, cosine, sine):
-    return tile * cosine - (sign * sine) * roll_rows(tile, 4)
+    return jnp.where(sublane() % 4 < 2, 1.0, -1.0).astype(F32)
+
+
+def other_part(tile):
+    return jnp.where(sublane() % 4 < 2, roll_rows(tile, 6), roll_rows(tile, 2))
+
+
+def tile_turn(tile, cosine, signed_sine):
+    return tile * cosine - signed_sine * other_part(tile)
 
 
 def tile_fft(tiles, sign, direction):
@@ -122,23 +127,62 @@
     for k in range(size // 2):
         turned = odd[k]
         if 4 * k == size:
-            turned = (-direction * sign) * roll_rows(turned, 4)
+            turned = (-direction * sign) * other_part(turned)
         elif k:
             angle = direction * 2.0 * math.pi * k / size
-            turned = tile_turn(turned, sign, math.cos(angle), math.sin(angle))
+            turned = tile_turn(turned, math.cos(angle), sign * math.sin(angle))
         low.append(even[k] + turned)
         high.append(even[k] - turned)
     return low + high
 
 
-def dot3(values, high, low, dims):
-    dot = lambda a, b: lax.dot_general(a, b, (dims, ((), ())), preferred_element_type=F32)
+def second_turn(tile, k, sign, direction):
+    if k == 0:
+        return tile
+    angle = direction * 2.0 * math.pi * k / ROWS
+    lower = sublane() < 4
+    cosine = jnp.where(lower, 1.0, math.cos(angle)).astype(F32)
+    sine = jnp.where(lower, 0.0, math.sin(angle)).astype(F32)
+    return tile_turn(tile, cosine, sign * sine)
+
+
+def block_sums(tile):
+    return jnp.where(sublane() < 4, tile, -tile) + roll_rows(tile, 4)
+
+
+def fft_down(tiles, sign):
+    turned = [second_turn(x, k, sign, -1) for k, x in enumerate(tile_fft(tiles, sign, -1))]
+    return [block_sums(x) for x in turned]
+
+
+def fft_up(tiles, sign):
+    turned = [second_turn(block_sums(x), k, sign, 1) for k, x in enumerate(tiles)]
+    return tile_fft(turned, sign, 1)
+
+
+MATRIX = (((1,), (0,)), ((), ()))
+
+
+def pieces(values):
     top = values.astype(BF16)
-    rest = (values - top.astype(F32)).astype(BF16)
-    return dot(top, high) + (dot(rest, high) + dot(top, low))
-
-
-FORWARD = ((1,), (0,))
+    return top, (values - top.astype(F32)).astype(BF16)
+
+
+def dot_wide(values, high, low):
+    top, rest = pieces(values)
+    size = values.shape[0]
+    both = lax.dot_general(
+        jnp.concatenate([top, rest], axis=0), high, MATRIX, preferred_element_type=F32
+    )
+    corner = lax.dot_general(top, low, MATRIX, preferred_element_type=F32)
+    return both[:size] + (both[size:] + corner)
+
+
+def dot_tall(values, matrix):
+    top, rest = pieces(values)
+    return lax.dot_general(
+        jnp.concatenate([top, rest, top], axis=1), matrix, MATRIX, preferred_element_type=F32
+    )
 
 
 def forward_columns(values, turn_cos, turn_sin, weights):
@@ -150,22 +194,24 @@
         cosine, sine = turn_cos[k : k + 1, :], turn_sin[k : k + 1, :]
         rows.append(jnp.concatenate([re * cosine + im * sine, im * cosine - re * sine], axis=1))
     stacked = jnp.concatenate(rows, axis=0)
-    out = dot3(stacked, weights[0], weights[1], FORWARD)
-    first = dot3(stacked[:16], weights[2], weights[3], FORWARD)
-    blocks = []
+    out = dot_wide(stacked, weights[0], weights[1])
+    first = dot_wide(stacked[:16], weights[2], weights[3])
+    blocks = [[], []]
     for slot in range(COLS // 2):
         row = first[:8] if slot == 0 else out[8 * slot : 8 * slot + 8]
-        blocks += [row[:, :WIDE], row[:, WIDE:]]
+        for n in range(4):
+            blocks[n % 2].append(row[:, LANES * n : LANES * (n + 1)])
     return blocks
 
 
 def backward_columns(blocks, turn_cos, turn_sin, weights):
-    stacked = jnp.concatenate(
-        [jnp.concatenate([blocks[2 * s], blocks[2 * s + 1]], axis=1) for s in range(COLS // 2)],
-        axis=0,
-    )
-    out = dot3(stacked, weights[0], weights[1], FORWARD)
-    first = dot3(stacked[:16], weights[2], weights[3], FORWARD)
+    rows = []
+    for s in range(COLS // 2):
+        row = [blocks[0][2 * s], blocks[1][2 * s], blocks[0][2 * s + 1], blocks[1][2 * s + 1]]
+        rows.append(jnp.concatenate(row, axis=1))
+    stacked = jnp.concatenate(rows, axis=0)
+    out = dot_wide(stacked, weights[0], weights[1])
+    first = dot_wide(stacked[:16], weights[2], weights[3])
     spectrum = [None] * (COLS // 2)
     for k in range(1, COLS // 2):
         row = out[8 * k : 8 * k + 8]
@@ -190,12 +236,12 @@
     return growth, (growth - 1.0) / linear
 
 
-def factors(step, row, col):
-    column = sublane() % 4
-    slot, half = col // 2, col % 2
-    within = LANES * half + 4 * row + column
+def factors(step, half, row, col):
+    column = 2 * half + sublane() % 2
+    slot, side = col // 2, col % 2
+    within = LANES * side + 4 * row + column
     q = jnp.where(slot == 0, 8 * within, slot + COLS * within)
-    p = step + ROWS * lax.broadcasted_iota(jnp.int32, (8, LANES), 1)
+    p = step + TILES * (sublane() // 4) + ROWS * lax.broadcasted_iota(jnp.int32, (8, LANES), 1)
     row_wave = squared_wave(p)
     wave_number = row_wave + squared_wave(q)
     last = row_wave + (2.0 * math.pi * (TOTAL // 2)) ** 2
@@ -203,7 +249,7 @@
     paired = jnp.where(q == 0, 1.0, jnp.where(slot == 0, 2.0, 1.0)).astype(F32)
     out = []
     for species, sign in ((SUBSTRATE, -1.0), (ACTIVATOR, 1.0)):
-        for waves, scale in ((wave_number, paired * norm), (last, norm)):
+        for waves, scale in ((wave_number, paired * norm), (last, norm))[: 2 - half]:
             growth, forcing = growth_forcing(waves, *species)
             out += [growth * scale, forcing * (scale * sign)]
     return out
@@ -215,8 +261,8 @@
         return high, (matrix - high.astype(np.float64)).astype(np.float32).astype(BF16)
 
     def interleave(re, im):
-        size = re.shape[0]
-        return np.stack([re.reshape(size, -1, 4), im.reshape(size, -1, 4)], axis=2).reshape(size, -1)
+        both = np.stack([re, im], axis=1).reshape(-1, 2, 2, ROWS, 2, 2)
+        return both.transpose(0, 2, 4, 3, 1, 5).reshape(re.shape[0], -1)
 
     j = np.arange(WIDE)
     angle = 2.0 * np.pi * (np.outer(j, j) % WIDE) / WIDE
@@ -230,16 +276,20 @@
     wide = np.stack([*split(pair), *split(single)])
     i = np.arange(LANES)
     angle = 2.0 * np.pi * (np.outer(i, i) % LANES) / LANES
-    tall = np.stack(split(np.concatenate([np.cos(angle), np.sin(angle)], axis=1)))
-
-    def turns(count, size):
-        angle = 2.0 * np.pi * np.outer(np.arange(count), np.arange(size)) / TOTAL
-        return np.stack([np.cos(angle), np.sin(angle)]).astype(np.float32)
-
-    return wide, tall, turns(COLS // 2, WIDE), turns(ROWS, LANES)
-
-
-SEND1, SEND2, SEND3, SEND4, SEND5, SEND6 = 0, 2, 5, 8, 10, 12
+    high, low = split(np.concatenate([np.cos(angle), np.sin(angle)], axis=1))
+    tall = np.concatenate([high, high, low])
+
+    angle = 2.0 * np.pi * np.outer(np.arange(COLS // 2), j) / TOTAL
+    turn1 = np.stack([np.cos(angle), np.sin(angle)]).astype(np.float32)
+    block, part, _ = np.unravel_index(np.arange(8), (2, 2, 2))
+    wave = np.arange(TILES)[:, None] + TILES * block
+    angle = 2.0 * np.pi * wave[:, :, None] * i / TOTAL
+    sign = np.where(part == 0, 1.0, -1.0)[:, None]
+    turn2 = np.stack([np.cos(angle), sign * np.sin(angle)]).astype(np.float32)
+    return wide, tall, turn1, turn2
+
+
+SEND1, SEND2, SEND3, SEND4, SEND5, SEND6 = 0, 2, 8, 14, 18, 22
 U, R, V = 0, 1, 2
 
 
@@ -310,28 +360,31 @@
     greet("col", col, COLS)
     greet("row", row, ROWS)
     loads[0].wait()
-    loads[1].wait()
     pl.semaphore_wait(barrier, COLS - 1 + ROWS - 1)
 
     for n in range(2):
+        if n == 1:
+            loads[1].wait()
         send("col", fields.at[n], got1.at[n], SEND1 + n)
         got1[n, col] = fields[n, col]
 
     def fill(step, carry):
-        for n, table in enumerate(factors(step, row, col)):
-            tables[n, step] = table
+        for half in range(2):
+            for n, table in enumerate(factors(step, half, row, col)):
+                tables[8 * half + n, step] = table
         return carry
 
-    lax.fori_loop(0, ROWS, fill, 0)
+    lax.fori_loop(0, TILES, fill, 0)
 
     def forward_rows(n, values):
         blocks = forward_columns(
             values, turn1[0], turn1[1], [wide.at[k][...] for k in range(4)]
         )
-        for c in range(COLS):
-            put2[n, c] = blocks[c]
-        send("col", put2.at[n], got2.at[n], SEND2 + n)
-        got2[n, col] = put2[n, col]
+        for h in range(2):
+            for c in range(COLS):
+                put2[n, h, c] = blocks[h][c]
+            send("col", put2.at[n, h], got2.at[n, h], SEND2 + 2 * n + h)
+            got2[n, h, col] = put2[n, h, col]
 
     for load in loads[2:]:
         load.wait()
@@ -342,73 +395,88 @@
     forward_rows(V, [got1[1, c] for c in range(COLS)])
 
     for n in (U, R, V):
-        whole("col", got2.at[n], SEND2 + n).wait_recv()
-        block = got2[n].reshape(COLS * 8, WIDE)
-        put3[n] = block.T.reshape(ROWS, 8, LANES)
-        send("row", put3.at[n], got3.at[n], SEND3 + n)
-        got3[n, row] = put3[n, row]
+        for h in range(2):
+            whole("col", got2.at[n, h], SEND2 + 2 * n + h).wait_recv()
+            turned = got2[n, h].reshape(LANES, LANES).T
+            for r in range(ROWS):
+                put3[n, h, r] = turned[4 * r : 4 * r + 4]
+            send("row", put3.at[n, h], got3.at[n, h], SEND3 + 2 * n + h)
+            got3[n, h, row] = put3[n, h, row]
 
     sign = part_sign()
 
-    def forward_down(n):
-        whole("row", got3.at[n], SEND3 + n).wait_recv()
-        values = tile_fft([got3[n, r] for r in range(ROWS)], sign, -1)
-        for k in range(ROWS):
-            cosine, sine = turn2[0, k : k + 1, :], turn2[1, k : k + 1, :]
-            tiles[k] = tile_turn(values[k], sign, cosine, -sine)
-        out = dot3(tiles[...].reshape(ROWS * 8, LANES), tall[0], tall[1], FORWARD)
-        products[pl.ds(0, ROWS)] = out.reshape(ROWS, 8, 2 * LANES)
-        for k in range(ROWS):
+    def two_blocks(ref, t):
+        return jnp.concatenate([ref[2 * t], ref[2 * t + 1]], axis=0)
+
+    def forward_down(n, h):
+        whole("row", got3.at[n, h], SEND3 + 2 * n + h).wait_recv()
+        values = fft_down([two_blocks(got3.at[n, h], t) for t in range(TILES)], sign)
+        for k in range(TILES):
+            tiles[k] = tile_turn(values[k], turn2[0, k], -turn2[1, k])
+        out = dot_tall(tiles[...].reshape(LANES, LANES), tall[...])
+        products[pl.ds(0, TILES)] = out.reshape(TILES, 8, 2 * LANES)
+        for k in range(TILES):
             both = products[k]
-            spectra[n, k] = both[:, :LANES] + sign * roll_rows(both[:, LANES:], 4)
-
-    special = sublane() == jnp.where(row + col == 0, 4, -1)
-
-    def backward_down(n, field):
-        for k in range(ROWS):
-            own, source = spectra[field, k], spectra[R, k]
-            for m in range(2):
-                t = 4 * n + 2 * m
-                pair[m * ROWS + k] = tables[t, k] * own + tables[t + 1, k] * source
-        block = pair[...].reshape(2 * ROWS * 8, LANES)
-        products[...] = dot3(block, tall[0], tall[1], FORWARD).reshape(2 * ROWS, 8, 2 * LANES)
-        for m in (1, 0):
+            spectra[n, h, k] = both[:, :LANES] + sign * other_part(both[:, LANES:])
+
+    special = sublane() % 4 == jnp.where(row + col == 0, 2, -1)
+
+    def backward_down(n, field, h):
+        parts = 2 - h
+        for k in range(TILES):
+            own, source = spectra[field, h, k], spectra[R, h, k]
+            for m in range(parts):
+                t = 8 * h + 2 * (parts * n + m)
+                pair[m * TILES + k] = tables[t, k] * own + tables[t + 1, k] * source
+        block = pair[pl.ds(0, parts * TILES)].reshape(parts * LANES, LANES)
+        out = dot_tall(block, tall[...])
+        products[pl.ds(0, parts * TILES)] = out.reshape(parts * TILES, 8, 2 * LANES)
+        for m in reversed(range(parts)):
             turned = []
-            for k in range(ROWS):
-                both = products[m * ROWS + k]
-                tile = both[:, :LANES] - sign * roll_rows(both[:, LANES:], 4)
-                cosine, sine = turn2[0, k : k + 1, :], turn2[1, k : k + 1, :]
-                turned.append(tile_turn(tile, sign, cosine, sine))
-            values = tile_fft(turned, sign, 1)
-            for r in range(ROWS):
+            for k in range(TILES):
+                both = products[m * TILES + k]
+                tile = both[:, :LANES] - sign * other_part(both[:, LANES:])
+                turned.append(tile_turn(tile, turn2[0, k], turn2[1, k]))
+            values = fft_up(turned, sign)
+            for t in range(TILES):
+                value = values[t]
                 if m == 1:
-                    tiles[r] = values[r]
-                else:
-                    put4[n, r] = jnp.where(special, tiles[r], values[r])
-        send("row", put4.at[n], got4.at[n], SEND4 + n)
-        got4[n, row] = put4[n, row]
-
-    forward_down(U)
-    forward_down(R)
-    backward_down(0, U)
-    forward_down(V)
-    backward_down(1, V)
+                    tiles[t] = value
+                    continue
+                if h == 0:
+                    value = jnp.where(special, tiles[t], value)
+                put4[n, h, 2 * t] = value[:4]
+                put4[n, h, 2 * t + 1] = value[4:]
+        send("row", put4.at[n, h], got4.at[n, h], SEND4 + 2 * n + h)
+        got4[n, h, row] = put4[n, h, row]
+
+    forward_down(U, 0)
+    forward_down(U, 1)
+    for h in range(2):
+        forward_down(R, h)
+        backward_down(0, U, h)
+    for h in range(2):
+        forward_down(V, h)
+        backward_down(1, V, h)
 
     for k in range(4):
         back[k] = wide.at[k][...].T
 
     for n in range(2):
-        whole("row", got4.at[n], SEND4 + n).wait_recv()
-        block = got4[n].reshape(ROWS * 8, LANES)
-        put5[n] = block.T.reshape(COLS, 8, WIDE)
-        send("col", put5.at[n], got5.at[n], SEND5 + n)
-        got5[n, col] = put5[n, col]
+        for h in range(2):
+            whole("row", got4.at[n, h], SEND4 + 2 * n + h).wait_recv()
+            block = jnp.concatenate([two_blocks(got4.at[n, h], t) for t in range(TILES)], axis=0)
+            put5[n, h] = block.T.reshape(COLS, 8, LANES)
+            send("col", put5.at[n, h], got5.at[n, h], SEND5 + 2 * n + h)
+            got5[n, h, col] = put5[n, h, col]
 
     _, feed = growth_forcing_at_zero()
     for n, out in enumerate((s_out, a_out)):
-        whole("col", got5.at[n], SEND5 + n).wait_recv()
+        for h in range(2):
+            whole("col", got5.at[n, h], SEND5 + 2 * n + h).wait_recv()
         weights = [back.at[k][...] for k in range(4)]
-        values = backward_columns([got5[n, c] for c in range(COLS)], turn1[0], turn1[1], weights)
+        blocks = [[got5[n, h, c] for c in range(COLS)] for h in range(2)]
+        values = backward_columns(blocks, turn1[0], turn1[1], weights)
         for c in range(COLS):
             put6[n, c] = values[c] + feed if n == 0 else values[c]
         send("col", put6.at[n], out, SEND6 + n)
@@ -431,7 +499,8 @@
     held = lambda x: pltpu.with_memory_space_constraint(x, pltpu.HBM)
     anywhere = pl.BlockSpec(memory_space=pltpu.HBM)
     vmem = lambda *shape: pltpu.VMEM(shape, F32)
-    by_col, by_row = (COLS, 8, WIDE), (ROWS, 8, LANES)
+    by_col, by_tile = (COLS, 8, WIDE), (TILES, 8, LANES)
+    half_col, half_row = (2, COLS, 8, LANES), (2, ROWS, 4, LANES)
     out = pl.pallas_call(
         kernel,
         name="section",
@@ -444,25 +513,25 @@
             pltpu.VMEM(tall.shape, BF16),
             vmem(*turn1.shape),
             vmem(*turn2.shape),
-            vmem(8, *by_row),
+            vmem(16, *by_tile),
             pltpu.VMEM(wide.shape, BF16),
             vmem(2, *by_col),
-            vmem(3, *by_col),
-            vmem(3, *by_col),
-            vmem(3, *by_row),
-            vmem(3, *by_row),
-            vmem(*by_row),
-            vmem(3, *by_row),
-            vmem(2 * ROWS, 8, LANES),
-            vmem(2 * ROWS, 8, 2 * LANES),
-            vmem(2, *by_row),
-            vmem(2, *by_row),
-            vmem(2, *by_col),
-            vmem(2, *by_col),
+            vmem(3, *half_col),
+            vmem(3, *half_col),
+            vmem(3, *half_row),
+            vmem(3, *half_row),
+            vmem(*by_tile),
+            vmem(3, 2, *by_tile),
+            vmem(2 * TILES, 8, LANES),
+            vmem(2 * TILES, 8, 2 * LANES),
+            vmem(2, *half_row),
+            vmem(2, *half_row),
+            vmem(2, *half_col),
+            vmem(2, *half_col),
             vmem(2, *by_col),
             pltpu.SemaphoreType.DMA((6,)),
-            pltpu.SemaphoreType.DMA((14,)),
-            pltpu.SemaphoreType.DMA((14,)),
+            pltpu.SemaphoreType.DMA((24,)),
+            pltpu.SemaphoreType.DMA((24,)),
         ],
         compiler_params=pltpu.CompilerParams(
             collective_id=0, has_side_effects=True, vmem_limit_bytes=20 << 20

time: 71 us -> 65.7 us (0.925)
  Pallas kernels: 68.7 us -> 63.5 us
    pallas_call x1, Pallas kernels: 68.7 us -> 63.5 us  [on_device(): pl.pallas_call(kernel, name='section', out_shape=(shape, shape), in_specs...]
where the time goes in v3:
time: 65.7 us; the launch traced here: 65.4 us
  Pallas kernels  63.5 us (97%)
  local copies, waits for them, and re-layouts  1.31 us (2%)
    pallas_call x1, Pallas kernels, on_device(): pl.pallas_call(kernel, name='section', out_shape=(shape, shape), in_specs...  63.5 us

profile of v3, /device:TPU:1, one launch (start us, length us, event | category | flops | bytes accessed | tf_op | source)
XLA Modules:
  0.0 65.4 jit_solution(7376318753700219137)
XLA Ops:
  0.6 63.5 %section.1 = (f32[16,8,256]{2,1,0:T(8,128)S(1)}, f32[16,8,256]{2,1,0:T(8,128)S(1)}) custom-call(f32[16,8,256]{2,1,0:T(8,128)} %bitcast.6, f32[16,8,256]{2,1,0:T(8,128)} %bitcast.7, bf16[4,512,512]{2,1,0:T(8,128)(2,1)} %constant.8.clone.wide_hbm, bf16[384,256]{1,0:T(8,128)(2,1)} %constant.9.clone.tall_hbm, f32[2,8,256]{2,1,0:T(8,128)} %constant.10.clone.turn1_hbm, ...), custom_call_target="tpu_custom_call" | custom-call | tf_op jit(solution)/shard_map/section/pallas_call | solution.py:504
  64.1 0.7 %copy.10 = f32[128,256]{1,0:T(8,128)} copy(f32[128,256]{1,0:T(8,128)S(1)} %bitcast.5) | data formatting | bytes 262144
  64.8 0.7 %copy.11 = f32[128,256]{1,0:T(8,128)} copy(f32[128,256]{1,0:T(8,128)S(1)} %bitcast.4) | data formatting | bytes 262144

commit v4 on v3

--- a/solution.py
+++ b/solution.py
@@ -321,13 +321,12 @@
     barrier = pltpu.get_barrier_semaphore()
 
     def greet(axis, me, size):
-        def body(k, carry):
-            pl.semaphore_signal(
-                barrier, inc=1, device_id={axis: lax.rem(me + k, size)}, device_id_type=mesh_id
-            )
+        def body(peer, carry):
+            pl.semaphore_signal(barrier, inc=1, device_id={axis: peer}, device_id_type=mesh_id)
             return carry
 
-        lax.fori_loop(1, size, body, 0)
+        lax.fori_loop(me + 1, size, body, 0)
+        lax.fori_loop(0, me, body, 0)
 
     pending = []
 
@@ -344,12 +343,12 @@
     def send(axis, source, target, sem):
         me, size = (col, COLS) if axis == "col" else (row, ROWS)
 
-        def body(k, carry):
-            peer = lax.rem(me + k, size)
+        def body(peer, carry):
             piece(axis, peer, source.at[peer], target.at[me], sem).start()
             return carry
 
-        lax.fori_loop(1, size, body, 0)
+        lax.fori_loop(me + 1, size, body, 0)
+        lax.fori_loop(0, me, body, 0)
         pending.append((axis, source, sem))
 
     def whole(axis, block, sem):
@@ -486,6 +485,17 @@
         whole("col", out, SEND6 + n).wait_recv()
     for entry in pending:
         whole(*entry).wait_send()
+
+
+def store_kernel(s_ref, a_ref, s_out, a_out, sems):
+    copies = [
+        pltpu.make_async_copy(s_ref, s_out, sems.at[0]),
+        pltpu.make_async_copy(a_ref, a_out, sems.at[1]),
+    ]
+    for copy in copies:
+        copy.start()
+    for copy in copies:
+        copy.wait()
 
 
 def growth_forcing_at_zero():
@@ -544,7 +554,15 @@
         held(jnp.asarray(turn1)),
         held(jnp.asarray(turn2)),
     )
-    return tuple(x.reshape(substrate.shape) for x in out)
+    flat = jax.ShapeDtypeStruct(substrate.shape, F32)
+    return pl.pallas_call(
+        store_kernel,
+        name="store",
+        out_shape=(flat, flat),
+        in_specs=[pl.BlockSpec(memory_space=pltpu.VMEM)] * 2,
+        out_specs=(pl.BlockSpec(memory_space=pltpu.HBM),) * 2,
+        scratch_shapes=[pltpu.SemaphoreType.DMA((2,))],
+    )(*(pltpu.with_memory_space_constraint(x.reshape(substrate.shape), pltpu.VMEM) for x in out))
 
 
 def solution(mesh):

time: 65.7 us -> 65.1 us (level)
  local copies, waits for them, and re-layouts: 1.31 us -> 0 us
    unnamed x2 -> x0, local copies, waits for them, and re-layouts: 1.31 us -> none
    pallas_call x0 -> x1, Pallas kernels: none -> 0.72 us  [on_device(): pl.pallas_call(store_kernel, name='store', out_shape=(flat, flat), in_spe...]
where the time goes in v4:
time: 65.1 us; the launch traced here: 64.5 us
  Pallas kernels  63.8 us (98%)
    pallas_call x1, Pallas kernels, on_device(): pl.pallas_call(kernel, name='section', out_shape=(shape, shape), in_specs...  63.1 us

profile of v4, /device:TPU:1, one launch (start us, length us, event | category | flops | bytes accessed | tf_op | source)
XLA Modules:
  0.0 64.5 jit_solution(11646826343475486056)
XLA Ops:
  0.6 63.1 %section.1 = (f32[16,8,256]{2,1,0:T(8,128)S(1)}, f32[16,8,256]{2,1,0:T(8,128)S(1)}) custom-call(f32[16,8,256]{2,1,0:T(8,128)} %bitcast.6, f32[16,8,256]{2,1,0:T(8,128)} %bitcast.7, bf16[4,512,512]{2,1,0:T(8,128)(2,1)} %constant.8.clone.wide_hbm, bf16[384,256]{1,0:T(8,128)(2,1)} %constant.9.clone.tall_hbm, f32[2,8,256]{2,1,0:T(8,128)} %constant.10.clone.turn1_hbm, ...), custom_call_target="tpu_custom_call" | custom-call | tf_op jit(solution)/shard_map/section/pallas_call | solution.py:514
  63.8 0.7 %store.1 = (f32[128,256]{1,0:T(8,128)}, f32[128,256]{1,0:T(8,128)}) custom-call(f32[128,256]{1,0:T(8,128)S(1)} %bitcast.4, f32[128,256]{1,0:T(8,128)S(1)} %bitcast.5), custom_call_target="tpu_custom_call" | custom-call | tf_op jit(solution)/shard_map/store/pallas_call | solution.py:558

commit v5 on v4

--- a/solution.py
+++ b/solution.py
@@ -196,19 +196,14 @@
     stacked = jnp.concatenate(rows, axis=0)
     out = dot_wide(stacked, weights[0], weights[1])
     first = dot_wide(stacked[:16], weights[2], weights[3])
-    blocks = [[], []]
-    for slot in range(COLS // 2):
-        row = first[:8] if slot == 0 else out[8 * slot : 8 * slot + 8]
-        for n in range(4):
-            blocks[n % 2].append(row[:, LANES * n : LANES * (n + 1)])
-    return blocks
-
-
-def backward_columns(blocks, turn_cos, turn_sin, weights):
+    return [first[:8]] + [out[8 * slot : 8 * slot + 8] for slot in range(1, COLS // 2)]
+
+
+def backward_columns(blocks, added, turn_cos, turn_sin, weights):
     rows = []
     for s in range(COLS // 2):
         row = [blocks[0][2 * s], blocks[1][2 * s], blocks[0][2 * s + 1], blocks[1][2 * s + 1]]
-        rows.append(jnp.concatenate(row, axis=1))
+        rows.append(jnp.concatenate(row, axis=1) + added[s])
     stacked = jnp.concatenate(rows, axis=0)
     out = dot_wide(stacked, weights[0], weights[1])
     first = dot_wide(stacked[:16], weights[2], weights[3])
@@ -230,29 +225,35 @@
     return angular * angular
 
 
-def growth_forcing(wave_number, diffusion, decay_rate):
+def forcing_of(wave_number, diffusion, decay_rate):
     linear = -diffusion * wave_number - decay_rate
-    growth = jnp.exp(HALF_STEP * linear)
-    return growth, (growth - 1.0) / linear
-
-
-def factors(step, half, row, col):
-    column = 2 * half + sublane() % 2
+    return (jnp.exp(HALF_STEP * linear) - 1.0) / linear
+
+
+def forcings(step, half, row, col):
+    column = sublane() % 2
     slot, side = col // 2, col % 2
-    within = LANES * side + 4 * row + column
+    within = LANES * side + 4 * row + 2 * half + column
     q = jnp.where(slot == 0, 8 * within, slot + COLS * within)
     p = step + TILES * (sublane() // 4) + ROWS * lax.broadcasted_iota(jnp.int32, (8, LANES), 1)
     row_wave = squared_wave(p)
     wave_number = row_wave + squared_wave(q)
-    last = row_wave + (2.0 * math.pi * (TOTAL // 2)) ** 2
     norm = 1.0 / (TOTAL * TOTAL)
-    paired = jnp.where(q == 0, 1.0, jnp.where(slot == 0, 2.0, 1.0)).astype(F32)
-    out = []
-    for species, sign in ((SUBSTRATE, -1.0), (ACTIVATOR, 1.0)):
-        for waves, scale in ((wave_number, paired * norm), (last, norm))[: 2 - half]:
-            growth, forcing = growth_forcing(waves, *species)
-            out += [growth * scale, forcing * (scale * sign)]
+    scale = jnp.where(q == 0, norm, jnp.where(slot == 0, 2.0 * norm, norm)).astype(F32)
+    out = [
+        -scale * forcing_of(wave_number, *SUBSTRATE),
+        scale * forcing_of(wave_number, *ACTIVATOR),
+    ]
+    if half == 0:
+        last = row_wave + (2.0 * math.pi * (TOTAL // 2)) ** 2
+        first = -norm * forcing_of(last, *SUBSTRATE)
+        out.append(jnp.where(column == 0, first, norm * forcing_of(last, *ACTIVATOR)))
     return out
+
+
+def column_growth(index, diffusion):
+    angular = 2.0 * np.pi * np.where(2 * index < TOTAL, index, index - TOTAL)
+    return np.exp(-HALF_STEP * diffusion * angular * angular)
 
 
 def constants():
@@ -286,18 +287,36 @@
     angle = 2.0 * np.pi * wave[:, :, None] * i / TOTAL
     sign = np.where(part == 0, 1.0, -1.0)[:, None]
     turn2 = np.stack([np.cos(angle), sign * np.sin(angle)]).astype(np.float32)
-    return wide, tall, turn1, turn2
-
-
-SEND1, SEND2, SEND3, SEND4, SEND5, SEND6 = 0, 2, 8, 14, 18, 22
-U, R, V = 0, 1, 2
+    rows = np.arange(ROWS)[:, None] + ROWS * i
+    angle = 2.0 * np.pi * np.arange(ROWS)[:, None] * i / TOTAL
+    down = [np.cos(angle), np.sin(angle)]
+    slot = np.arange(COLS // 2)[:, None]
+    q = np.where(slot == 0, 8 * j, slot + COLS * j)
+    last = np.where(q == 0, TOTAL // 2, q)
+    paired = np.where(slot == 0, 2.0, 1.0)
+    across = []
+    for diffusion, decay_rate in (SUBSTRATE, ACTIVATOR):
+        down.append(column_growth(rows, diffusion) / TOTAL)
+        decay = math.exp(-HALF_STEP * decay_rate) / TOTAL
+        parts = [
+            np.where(q == 0, 1.0, paired) * column_growth(waves, diffusion) * decay
+            for waves in (q, last)
+        ]
+        across.append(interleave(*parts))
+    down, across = np.stack(down).astype(np.float32), np.stack(across).astype(np.float32)
+    return wide, tall, turn1, turn2, down, across
+
+
+SEND1, SEND2, SEND3, SEND4, SEND5, SEND6 = 0, 1, 3, 5, 9, 13
+SENDA, SENDB, SENDC = 15, 17, 19
 
 
 def kernel(
-    u_hbm, v_hbm, wide_hbm, tall_hbm, turn1_hbm, turn2_hbm, s_out, a_out,
-    fields, wide, tall, turn1, turn2, tables, back,
-    got1, put2, got2, put3, got3, tiles, spectra, pair, products,
-    put4, got4, put5, got5, put6, local_sem, send_sem, recv_sem,
+    u_hbm, v_hbm, wide_hbm, tall_hbm, turn1_hbm, turn2_hbm, down_hbm, across_hbm, s_out, a_out,
+    fields, wide, tall, turn1, turn2, down, across, tables, back,
+    got1, put2, got2, put3, got3, tiles, spectra, pair, products, extra,
+    put4, got4, put5, got5, put6,
+    put_a, got_a, put_b, got_b, put_c, got_c, grown, local_sem, send_sem, recv_sem,
 ):
     row, col = lax.axis_index("row"), lax.axis_index("col")
     mesh_id = pl.DeviceIdType.MESH
@@ -312,6 +331,8 @@
                 (tall_hbm, tall),
                 (turn1_hbm, turn1),
                 (turn2_hbm, turn2),
+                (down_hbm, down),
+                (across_hbm, across),
             ]
         )
     ]
@@ -359,74 +380,113 @@
     greet("col", col, COLS)
     greet("row", row, ROWS)
     loads[0].wait()
+    loads[1].wait()
+    fields[2] = fields[0] * fields[1] * fields[1]
     pl.semaphore_wait(barrier, COLS - 1 + ROWS - 1)
 
+    sign = part_sign()
+
+    send("col", fields.at[2], got1, SEND1)
+    got1[col] = fields[2, col]
+
     for n in range(2):
-        if n == 1:
-            loads[1].wait()
-        send("col", fields.at[n], got1.at[n], SEND1 + n)
-        got1[n, col] = fields[n, col]
+        put_a[n] = fields[n].reshape(LANES, WIDE).T.reshape(ROWS, 8, LANES)
+        send("row", put_a.at[n], got_a.at[n], SENDA + n)
+        got_a[n, row] = put_a[n, row]
 
     def fill(step, carry):
         for half in range(2):
-            for n, table in enumerate(factors(step, half, row, col)):
-                tables[8 * half + n, step] = table
+            for n, table in enumerate(forcings(step, half, row, col)):
+                tables[3 * half + n, step] = table
         return carry
 
     lax.fori_loop(0, TILES, fill, 0)
-
-    def forward_rows(n, values):
-        blocks = forward_columns(
-            values, turn1[0], turn1[1], [wide.at[k][...] for k in range(4)]
-        )
-        for h in range(2):
-            for c in range(COLS):
-                put2[n, h, c] = blocks[h][c]
-            send("col", put2.at[n, h], got2.at[n, h], SEND2 + 2 * n + h)
-            got2[n, h, col] = put2[n, h, col]
-
     for load in loads[2:]:
         load.wait()
-    whole("col", got1.at[0], SEND1).wait_recv()
-    forward_rows(U, [got1[0, c] for c in range(COLS)])
-    whole("col", got1.at[1], SEND1 + 1).wait_recv()
-    forward_rows(R, [got1[0, c] * got1[1, c] * got1[1, c] for c in range(COLS)])
-    forward_rows(V, [got1[1, c] for c in range(COLS)])
-
-    for n in (U, R, V):
-        for h in range(2):
-            whole("col", got2.at[n, h], SEND2 + 2 * n + h).wait_recv()
-            turned = got2[n, h].reshape(LANES, LANES).T
-            for r in range(ROWS):
-                put3[n, h, r] = turned[4 * r : 4 * r + 4]
-            send("row", put3.at[n, h], got3.at[n, h], SEND3 + 2 * n + h)
-            got3[n, h, row] = put3[n, h, row]
-
-    sign = part_sign()
+
+    def spectrum_of(values):
+        weights = [wide.at[k][...] for k in range(4)]
+        return forward_columns(values, turn1[0], turn1[1], weights)
+
+    whole("col", got1, SEND1).wait_recv()
+    rows = spectrum_of([got1[c] for c in range(COLS)])
+    for h in range(2):
+        for c in range(COLS):
+            start = WIDE * (c % 2) + LANES * h
+            put2[h, c] = rows[c // 2][:, start : start + LANES]
+        send("col", put2.at[h], got2.at[h], SEND2 + h)
+        got2[h, col] = put2[h, col]
+
+    def filter_columns(n):
+        whole("row", got_a.at[n], SENDA + n).wait_recv()
+        values = tile_fft([got_a[n, r] for r in range(ROWS)], sign, -1)
+        for k in range(ROWS):
+            cosine, sine = down[0, k : k + 1, :], sign * down[1, k : k + 1, :]
+            pair[k] = tile_turn(values[k], cosine, -sine)
+        out = dot_tall(pair[...].reshape(ROWS * 8, LANES), tall[...])
+        products[pl.ds(0, ROWS)] = out.reshape(ROWS, 8, 2 * LANES)
+        for k in range(ROWS):
+            both = products[k]
+            wave = both[:, :LANES] + sign * other_part(both[:, LANES:])
+            pair[k] = wave * down[2 + n, k : k + 1, :]
+        out = dot_tall(pair[...].reshape(ROWS * 8, LANES), tall[...])
+        products[pl.ds(0, ROWS)] = out.reshape(ROWS, 8, 2 * LANES)
+        turned = []
+        for k in range(ROWS):
+            both = products[k]
+            tile = both[:, :LANES] - sign * other_part(both[:, LANES:])
+            cosine, sine = down[0, k : k + 1, :], sign * down[1, k : k + 1, :]
+            turned.append(tile_turn(tile, cosine, sine))
+        values = tile_fft(turned, sign, 1)
+        for r in range(ROWS):
+            put_b[n, r] = values[r]
+        send("row", put_b.at[n], got_b.at[n], SENDB + n)
+        got_b[n, row] = put_b[n, row]
+
+    def send_rows(n):
+        whole("row", got_b.at[n], SENDB + n).wait_recv()
+        put_c[n] = got_b[n].reshape(WIDE, LANES).T.reshape(COLS, 8, WIDE)
+        send("col", put_c.at[n], got_c.at[n], SENDC + n)
+        got_c[n, col] = put_c[n, col]
+
+    def grow(n):
+        whole("col", got_c.at[n], SENDC + n).wait_recv()
+        rows = spectrum_of([got_c[n, c] for c in range(COLS)])
+        for s in range(COLS // 2):
+            grown[n, s] = rows[s] * across[n, s : s + 1, :]
+
+    def turn_columns(h):
+        whole("col", got2.at[h], SEND2 + h).wait_recv()
+        turned = got2[h].reshape(LANES, LANES).T
+        for r in range(ROWS):
+            put3[h, r] = turned[4 * r : 4 * r + 4]
+        send("row", put3.at[h], got3.at[h], SEND3 + h)
+        got3[h, row] = put3[h, row]
 
     def two_blocks(ref, t):
         return jnp.concatenate([ref[2 * t], ref[2 * t + 1]], axis=0)
 
-    def forward_down(n, h):
-        whole("row", got3.at[n, h], SEND3 + 2 * n + h).wait_recv()
-        values = fft_down([two_blocks(got3.at[n, h], t) for t in range(TILES)], sign)
+    def forward_down(h):
+        whole("row", got3.at[h], SEND3 + h).wait_recv()
+        values = fft_down([two_blocks(got3.at[h], t) for t in range(TILES)], sign)
         for k in range(TILES):
             tiles[k] = tile_turn(values[k], turn2[0, k], -turn2[1, k])
         out = dot_tall(tiles[...].reshape(LANES, LANES), tall[...])
         products[pl.ds(0, TILES)] = out.reshape(TILES, 8, 2 * LANES)
         for k in range(TILES):
             both = products[k]
-            spectra[n, h, k] = both[:, :LANES] + sign * other_part(both[:, LANES:])
+            spectra[h, k] = both[:, :LANES] + sign * other_part(both[:, LANES:])
 
     special = sublane() % 4 == jnp.where(row + col == 0, 2, -1)
 
-    def backward_down(n, field, h):
-        parts = 2 - h
+    def backward_down(n, h):
+        parts = 2 if n == 0 and h == 0 else 1
         for k in range(TILES):
-            own, source = spectra[field, h, k], spectra[R, h, k]
-            for m in range(parts):
-                t = 8 * h + 2 * (parts * n + m)
-                pair[m * TILES + k] = tables[t, k] * own + tables[t + 1, k] * source
+            wave = spectra[h, k]
+            pair[k] = tables[3 * h + n, k] * wave
+            if parts == 2:
+                both = jnp.where(sublane() % 2 == 0, wave, roll_rows(wave, 1))
+                pair[TILES + k] = tables[2, k] * both
         block = pair[pl.ds(0, parts * TILES)].reshape(parts * LANES, LANES)
         out = dot_tall(block, tall[...])
         products[pl.ds(0, parts * TILES)] = out.reshape(parts * TILES, 8, 2 * LANES)
@@ -440,42 +500,51 @@
             for t in range(TILES):
                 value = values[t]
                 if m == 1:
-                    tiles[t] = value
+                    extra[t] = value
                     continue
                 if h == 0:
-                    value = jnp.where(special, tiles[t], value)
+                    fixed = extra[t] if n == 0 else roll_rows(extra[t], 7)
+                    value = jnp.where(special, fixed, value)
                 put4[n, h, 2 * t] = value[:4]
                 put4[n, h, 2 * t + 1] = value[4:]
         send("row", put4.at[n, h], got4.at[n, h], SEND4 + 2 * n + h)
         got4[n, h, row] = put4[n, h, row]
 
-    forward_down(U, 0)
-    forward_down(U, 1)
-    for h in range(2):
-        forward_down(R, h)
-        backward_down(0, U, h)
-    for h in range(2):
-        forward_down(V, h)
-        backward_down(1, V, h)
-
+    def turn_back(n, h):
+        whole("row", got4.at[n, h], SEND4 + 2 * n + h).wait_recv()
+        block = jnp.concatenate([two_blocks(got4.at[n, h], t) for t in range(TILES)], axis=0)
+        put5[n, h] = block.T.reshape(COLS, 8, LANES)
+        send("col", put5.at[n, h], got5.at[n, h], SEND5 + 2 * n + h)
+        got5[n, h, col] = put5[n, h, col]
+
+    filter_columns(0)
+    filter_columns(1)
     for k in range(4):
         back[k] = wide.at[k][...].T
-
+    turn_columns(0)
+    turn_columns(1)
+    send_rows(0)
+    forward_down(0)
+    backward_down(0, 0)
+    forward_down(1)
+    backward_down(0, 1)
+    send_rows(1)
+    backward_down(1, 0)
+    backward_down(1, 1)
+    grow(0)
     for n in range(2):
         for h in range(2):
-            whole("row", got4.at[n, h], SEND4 + 2 * n + h).wait_recv()
-            block = jnp.concatenate([two_blocks(got4.at[n, h], t) for t in range(TILES)], axis=0)
-            put5[n, h] = block.T.reshape(COLS, 8, LANES)
-            send("col", put5.at[n, h], got5.at[n, h], SEND5 + 2 * n + h)
-            got5[n, h, col] = put5[n, h, col]
-
-    _, feed = growth_forcing_at_zero()
+            turn_back(n, h)
+    grow(1)
+
+    feed = feed_forcing()
     for n, out in enumerate((s_out, a_out)):
         for h in range(2):
             whole("col", got5.at[n, h], SEND5 + 2 * n + h).wait_recv()
         weights = [back.at[k][...] for k in range(4)]
         blocks = [[got5[n, h, c] for c in range(COLS)] for h in range(2)]
-        values = backward_columns(blocks, turn1[0], turn1[1], weights)
+        added = [grown[n, s] for s in range(COLS // 2)]
+        values = backward_columns(blocks, added, turn1[0], turn1[1], weights)
         for c in range(COLS):
             put6[n, c] = values[c] + feed if n == 0 else values[c]
         send("col", put6.at[n], out, SEND6 + n)
@@ -498,50 +567,61 @@
         copy.wait()
 
 
-def growth_forcing_at_zero():
+def feed_forcing():
     linear = -FEED_RATE
-    return math.exp(HALF_STEP * linear), FEED_RATE * math.expm1(HALF_STEP * linear) / linear
+    return FEED_RATE * math.expm1(HALF_STEP * linear) / linear
 
 
 def on_device(substrate, activator):
-    wide, tall, turn1, turn2 = constants()
+    wide, tall, turn1, turn2, down, across = constants()
     shape = pltpu.VMEM((COLS, 8, WIDE), F32)
     held = lambda x: pltpu.with_memory_space_constraint(x, pltpu.HBM)
     anywhere = pl.BlockSpec(memory_space=pltpu.HBM)
     vmem = lambda *shape: pltpu.VMEM(shape, F32)
     by_col, by_tile = (COLS, 8, WIDE), (TILES, 8, LANES)
+    by_row = (ROWS, 8, LANES)
     half_col, half_row = (2, COLS, 8, LANES), (2, ROWS, 4, LANES)
     out = pl.pallas_call(
         kernel,
         name="section",
         out_shape=(shape, shape),
-        in_specs=[anywhere] * 6,
+        in_specs=[anywhere] * 8,
         out_specs=(pl.BlockSpec(memory_space=pltpu.VMEM),) * 2,
         scratch_shapes=[
-            vmem(2, *by_col),
+            vmem(3, *by_col),
             pltpu.VMEM(wide.shape, BF16),
             pltpu.VMEM(tall.shape, BF16),
             vmem(*turn1.shape),
             vmem(*turn2.shape),
-            vmem(16, *by_tile),
+            vmem(*down.shape),
+            vmem(*across.shape),
+            vmem(5, *by_tile),
             pltpu.VMEM(wide.shape, BF16),
-            vmem(2, *by_col),
-            vmem(3, *half_col),
-            vmem(3, *half_col),
-            vmem(3, *half_row),
-            vmem(3, *half_row),
+            vmem(*by_col),
+            vmem(*half_col),
+            vmem(*half_col),
+            vmem(*half_row),
+            vmem(*half_row),
             vmem(*by_tile),
-            vmem(3, 2, *by_tile),
+            vmem(2, *by_tile),
             vmem(2 * TILES, 8, LANES),
             vmem(2 * TILES, 8, 2 * LANES),
+            vmem(*by_tile),
             vmem(2, *half_row),
             vmem(2, *half_row),
             vmem(2, *half_col),
             vmem(2, *half_col),
             vmem(2, *by_col),
-            pltpu.SemaphoreType.DMA((6,)),
-            pltpu.SemaphoreType.DMA((24,)),
-            pltpu.SemaphoreType.DMA((24,)),
+            vmem(2, *by_row),
+            vmem(2, *by_row),
+            vmem(2, *by_row),
+            vmem(2, *by_row),
+            vmem(2, *by_col),
+            vmem(2, *by_col),
+            vmem(2, COLS // 2, 8, 2 * WIDE),
+            pltpu.SemaphoreType.DMA((8,)),
+            pltpu.SemaphoreType.DMA((21,)),
+            pltpu.SemaphoreType.DMA((21,)),
         ],
         compiler_params=pltpu.CompilerParams(
             collective_id=0, has_side_effects=True, vmem_limit_bytes=20 << 20
@@ -553,6 +633,8 @@
         held(jnp.asarray(tall)),
         held(jnp.asarray(turn1)),
         held(jnp.asarray(turn2)),
+        held(jnp.asarray(down)),
+        held(jnp.asarray(across)),
     )
     flat = jax.ShapeDtypeStruct(substrate.shape, F32)
     return pl.pallas_call(

time: 65.1 us -> 62.3 us (0.957)
  Pallas kernels: 63.8 us -> 61.6 us
    pallas_call x1, Pallas kernels: 63.1 us -> 60.9 us  [on_device(): pl.pallas_call(kernel, name='section', out_shape=(shape, shape), in_specs...]
where the time goes in v5:
time: 62.3 us; the launch traced here: 62.2 us
  Pallas kernels  61.6 us (99%)
  between operations  0.64 us (1%)
    pallas_call x1, Pallas kernels, on_device(): pl.pallas_call(kernel, name='section', out_shape=(shape, shape), in_specs...  60.9 us

profile of v5, /device:TPU:1, one launch (start us, length us, event | category | flops | bytes accessed | tf_op | source)
XLA Modules:
  0.0 62.2 jit_solution(2068596757818958156)
XLA Ops:
  0.6 60.9 %section.1 = (f32[16,8,256]{2,1,0:T(8,128)S(1)}, f32[16,8,256]{2,1,0:T(8,128)S(1)}) custom-call(f32[16,8,256]{2,1,0:T(8,128)} %bitcast.6, f32[16,8,256]{2,1,0:T(8,128)} %bitcast.7, bf16[4,512,512]{2,1,0:T(8,128)(2,1)} %constant.12.clone.wide_hbm, bf16[384,256]{1,0:T(8,128)(2,1)} %constant.13.clone.tall_hbm, f32[2,8,256]{2,1,0:T(8,128)} %constant.14.clone.turn1_hbm, ...), custom_call_target="tpu_custom_call" | custom-call | tf_op jit(solution)/shard_map/section/pallas_call | solution.py:584
  61.5 0.7 %store.1 = (f32[128,256]{1,0:T(8,128)}, f32[128,256]{1,0:T(8,128)}) custom-call(f32[128,256]{1,0:T(8,128)S(1)} %bitcast.4, f32[128,256]{1,0:T(8,128)S(1)} %bitcast.5), custom_call_target="tpu_custom_call" | custom-call | tf_op jit(solution)/shard_map/store/pallas_call | solution.py:640

commit v6 on v5

--- a/solution.py
+++ b/solution.py
@@ -185,7 +185,7 @@
     )
 
 
-def forward_columns(values, turn_cos, turn_sin, weights):
+def forward_columns(values, turn_cos, turn_sin):
     even, odd = real_forward(values[::2]), real_forward(values[1::2])
     spectrum = join_halves(even, odd, COLS, 1)
     rows = [jnp.concatenate([even[0][0], odd[0][0]], axis=1)]
@@ -193,28 +193,23 @@
         re, im = spectrum[k]
         cosine, sine = turn_cos[k : k + 1, :], turn_sin[k : k + 1, :]
         rows.append(jnp.concatenate([re * cosine + im * sine, im * cosine - re * sine], axis=1))
-    stacked = jnp.concatenate(rows, axis=0)
+    return jnp.concatenate(rows, axis=0)
+
+
+def half_product(stacked, weights):
     out = dot_wide(stacked, weights[0], weights[1])
     first = dot_wide(stacked[:16], weights[2], weights[3])
     return [first[:8]] + [out[8 * slot : 8 * slot + 8] for slot in range(1, COLS // 2)]
 
 
-def backward_columns(blocks, added, turn_cos, turn_sin, weights):
-    rows = []
-    for s in range(COLS // 2):
-        row = [blocks[0][2 * s], blocks[1][2 * s], blocks[0][2 * s + 1], blocks[1][2 * s + 1]]
-        rows.append(jnp.concatenate(row, axis=1) + added[s])
-    stacked = jnp.concatenate(rows, axis=0)
-    out = dot_wide(stacked, weights[0], weights[1])
-    first = dot_wide(stacked[:16], weights[2], weights[3])
+def backward_columns(products, turn_cos, turn_sin):
     spectrum = [None] * (COLS // 2)
     for k in range(1, COLS // 2):
-        row = out[8 * k : 8 * k + 8]
-        re, im = row[:, :WIDE], row[:, WIDE:]
+        re, im = products[k][:, :WIDE], products[k][:, WIDE:]
         cosine, sine = turn_cos[k : k + 1, :], turn_sin[k : k + 1, :]
         spectrum[k] = (re * cosine - im * sine, im * cosine + re * sine)
     even, odd = split_halves(spectrum + [None], COLS, 1)
-    even[0], odd[0] = (first[:8, :WIDE], None), (first[:8, WIDE:], None)
+    even[0], odd[0] = (products[0][:, :WIDE], None), (products[0][:, WIDE:], None)
     even, odd = real_backward(even), real_backward(odd)
     return [x for pair in zip(even, odd) for x in pair]
 
@@ -263,7 +258,7 @@
 
     def interleave(re, im):
         both = np.stack([re, im], axis=1).reshape(-1, 2, 2, ROWS, 2, 2)
-        return both.transpose(0, 2, 4, 3, 1, 5).reshape(re.shape[0], -1)
+        return both.transpose(0, 4, 2, 3, 1, 5).reshape(re.shape[0], -1)
 
     j = np.arange(WIDE)
     angle = 2.0 * np.pi * (np.outer(j, j) % WIDE) / WIDE
@@ -316,7 +311,7 @@
     fields, wide, tall, turn1, turn2, down, across, tables, back,
     got1, put2, got2, put3, got3, tiles, spectra, pair, products, extra,
     put4, got4, put5, got5, put6,
-    put_a, got_a, put_b, got_b, put_c, got_c, grown, local_sem, send_sem, recv_sem,
+    put_a, got_a, put_b, got_b, put_c, got_c, grown, partial, local_sem, send_sem, recv_sem,
 ):
     row, col = lax.axis_index("row"), lax.axis_index("col")
     mesh_id = pl.DeviceIdType.MESH
@@ -404,18 +399,21 @@
     for load in loads[2:]:
         load.wait()
 
-    def spectrum_of(values):
-        weights = [wide.at[k][...] for k in range(4)]
-        return forward_columns(values, turn1[0], turn1[1], weights)
+    def spectrum_of(values, keep):
+        stacked = forward_columns(values, turn1[0], turn1[1])
+        for h in range(2):
+            part = pl.ds(WIDE * h, WIDE)
+            keep(h, half_product(stacked, [wide[k, :, part] for k in range(4)]))
 
     whole("col", got1, SEND1).wait_recv()
-    rows = spectrum_of([got1[c] for c in range(COLS)])
-    for h in range(2):
+    def send_half(h, rows):
         for c in range(COLS):
-            start = WIDE * (c % 2) + LANES * h
+            start = LANES * (c % 2)
             put2[h, c] = rows[c // 2][:, start : start + LANES]
         send("col", put2.at[h], got2.at[h], SEND2 + h)
         got2[h, col] = put2[h, col]
+
+    spectrum_of([got1[c] for c in range(COLS)], send_half)
 
     def filter_columns(n):
         whole("row", got_a.at[n], SENDA + n).wait_recv()
@@ -451,9 +449,12 @@
 
     def grow(n):
         whole("col", got_c.at[n], SENDC + n).wait_recv()
-        rows = spectrum_of([got_c[n, c] for c in range(COLS)])
-        for s in range(COLS // 2):
-            grown[n, s] = rows[s] * across[n, s : s + 1, :]
+        def keep(h, rows):
+            part = pl.ds(WIDE * h, WIDE)
+            for s in range(COLS // 2):
+                grown[n, h, s] = rows[s] * across[n, s : s + 1, part]
+
+        spectrum_of([got_c[n, c] for c in range(COLS)], keep)
 
     def turn_columns(h):
         whole("col", got2.at[h], SEND2 + h).wait_recv()
@@ -518,11 +519,11 @@
         got5[n, h, col] = put5[n, h, col]
 
     filter_columns(0)
-    filter_columns(1)
     for k in range(4):
         back[k] = wide.at[k][...].T
     turn_columns(0)
     turn_columns(1)
+    filter_columns(1)
     send_rows(0)
     forward_down(0)
     backward_down(0, 0)
@@ -541,10 +542,20 @@
     for n, out in enumerate((s_out, a_out)):
         for h in range(2):
             whole("col", got5.at[n, h], SEND5 + 2 * n + h).wait_recv()
-        weights = [back.at[k][...] for k in range(4)]
-        blocks = [[got5[n, h, c] for c in range(COLS)] for h in range(2)]
-        added = [grown[n, s] for s in range(COLS // 2)]
-        values = backward_columns(blocks, added, turn1[0], turn1[1], weights)
+            rows = [
+                jnp.concatenate([got5[n, h, 2 * s], got5[n, h, 2 * s + 1]], axis=1) + grown[n, h, s]
+                for s in range(COLS // 2)
+            ]
+            weights = [back[k, pl.ds(WIDE * h, WIDE), :] for k in range(4)]
+            rows = half_product(jnp.concatenate(rows, axis=0), weights)
+            if h == 0:
+                for s in range(COLS // 2):
+                    partial[s] = rows[s]
+            else:
+                for s in range(COLS // 2):
+                    partial[s] = partial[s] + rows[s]
+        total = [partial[s] for s in range(COLS // 2)]
+        values = backward_columns(total, turn1[0], turn1[1])
         for c in range(COLS):
             put6[n, c] = values[c] + feed if n == 0 else values[c]
         send("col", put6.at[n], out, SEND6 + n)
@@ -618,7 +629,8 @@
             vmem(2, *by_row),
             vmem(2, *by_col),
             vmem(2, *by_col),
-            vmem(2, COLS // 2, 8, 2 * WIDE),
+            vmem(2, 2, COLS // 2, 8, WIDE),
+            vmem(COLS // 2, 8, 2 * WIDE),
             pltpu.SemaphoreType.DMA((8,)),
             pltpu.SemaphoreType.DMA((21,)),
             pltpu.SemaphoreType.DMA((21,)),

time: 62.3 us -> 61 us (0.979)
  Pallas kernels: 61.6 us -> 60.2 us
    pallas_call x1, Pallas kernels: 60.9 us -> 59.5 us  [on_device(): pl.pallas_call(kernel, name='section', out_shape=(shape, shape), in_specs...]
where the time goes in v6:
time: 61 us; the launch traced here: 60.8 us
  Pallas kernels  60.2 us (99%)
  between operations  0.64 us (1%)
    pallas_call x1, Pallas kernels, on_device(): pl.pallas_call(kernel, name='section', out_shape=(shape, shape), in_specs...  59.5 us

profile of v6, /device:TPU:1, one launch (start us, length us, event | category | flops | bytes accessed | tf_op | source)
XLA Modules:
  0.0 60.8 jit_solution(617510355044449805)
XLA Ops:
  0.6 59.5 %section.1 = (f32[16,8,256]{2,1,0:T(8,128)S(1)}, f32[16,8,256]{2,1,0:T(8,128)S(1)}) custom-call(f32[16,8,256]{2,1,0:T(8,128)} %bitcast.6, f32[16,8,256]{2,1,0:T(8,128)} %bitcast.7, bf16[4,512,512]{2,1,0:T(8,128)(2,1)} %constant.12.clone.wide_hbm, bf16[384,256]{1,0:T(8,128)(2,1)} %constant.13.clone.tall_hbm, f32[2,8,256]{2,1,0:T(8,128)} %constant.14.clone.turn1_hbm, ...), custom_call_target="tpu_custom_call" | custom-call | tf_op jit(solution)/shard_map/section/pallas_call | solution.py:595
  60.1 0.7 %store.1 = (f32[128,256]{1,0:T(8,128)}, f32[128,256]{1,0:T(8,128)}) custom-call(f32[128,256]{1,0:T(8,128)S(1)} %bitcast.4, f32[128,256]{1,0:T(8,128)S(1)} %bitcast.5), custom_call_target="tpu_custom_call" | custom-call | tf_op jit(solution)/shard_map/store/pallas_call | solution.py:652

commit v7 on v6

--- a/solution.py
+++ b/solution.py
@@ -180,9 +180,12 @@
 
 def dot_tall(values, matrix):
     top, rest = pieces(values)
-    return lax.dot_general(
-        jnp.concatenate([top, rest, top], axis=1), matrix, MATRIX, preferred_element_type=F32
-    )
+    stacked = jnp.concatenate([top, rest, top], axis=1)
+    parts = [
+        lax.dot_general(stacked, part, MATRIX, preferred_element_type=F32)
+        for part in (matrix[:, :LANES], matrix[:, LANES:])
+    ]
+    return jnp.concatenate(parts, axis=1)
 
 
 def forward_columns(values, turn_cos, turn_sin):
@@ -529,8 +532,8 @@
     backward_down(0, 0)
     forward_down(1)
     backward_down(0, 1)
+    backward_down(1, 0)
     send_rows(1)
-    backward_down(1, 0)
     backward_down(1, 1)
     grow(0)
     for n in range(2):

time: 61 us -> 60.5 us (level)
  no operation moved by 1% of the time
where the time goes in v7:
time: 60.5 us; the launch traced here: 60.4 us
  Pallas kernels  59.7 us (99%)
  between operations  0.64 us (1%)
    pallas_call x1, Pallas kernels, on_device(): pl.pallas_call(kernel, name='section', out_shape=(shape, shape), in_specs...  59 us

profile of v7, /device:TPU:1, one launch (start us, length us, event | category | flops | bytes accessed | tf_op | source)
XLA Modules:
  0.0 60.4 jit_solution(5325951615705547388)
XLA Ops:
  0.6 59.0 %section.1 = (f32[16,8,256]{2,1,0:T(8,128)S(1)}, f32[16,8,256]{2,1,0:T(8,128)S(1)}) custom-call(f32[16,8,256]{2,1,0:T(8,128)} %bitcast.6, f32[16,8,256]{2,1,0:T(8,128)} %bitcast.7, bf16[4,512,512]{2,1,0:T(8,128)(2,1)} %constant.12.clone.wide_hbm, bf16[384,256]{1,0:T(8,128)(2,1)} %constant.13.clone.tall_hbm, f32[2,8,256]{2,1,0:T(8,128)} %constant.14.clone.turn1_hbm, ...), custom_call_target="tpu_custom_call" | custom-call | tf_op jit(solution)/shard_map/section/pallas_call | solution.py:598
  59.6 0.7 %store.1 = (f32[128,256]{1,0:T(8,128)}, f32[128,256]{1,0:T(8,128)}) custom-call(f32[128,256]{1,0:T(8,128)S(1)} %bitcast.4, f32[128,256]{1,0:T(8,128)S(1)} %bitcast.5), custom_call_target="tpu_custom_call" | custom-call | tf_op jit(solution)/shard_map/store/pallas_call | solution.py:655

commit v8 on v7

--- a/solution.py
+++ b/solution.py
@@ -481,36 +481,41 @@
             both = products[k]
             spectra[h, k] = both[:, :LANES] + sign * other_part(both[:, LANES:])
 
-    special = sublane() % 4 == jnp.where(row + col == 0, 2, -1)
-
     def backward_down(n, h):
-        parts = 2 if n == 0 and h == 0 else 1
-        for k in range(TILES):
-            wave = spectra[h, k]
-            pair[k] = tables[3 * h + n, k] * wave
-            if parts == 2:
-                both = jnp.where(sublane() % 2 == 0, wave, roll_rows(wave, 1))
-                pair[TILES + k] = tables[2, k] * both
-        block = pair[pl.ds(0, parts * TILES)].reshape(parts * LANES, LANES)
-        out = dot_tall(block, tall[...])
-        products[pl.ds(0, parts * TILES)] = out.reshape(parts * TILES, 8, 2 * LANES)
-        for m in reversed(range(parts)):
+        def lifted(scaled):
+            for k in range(TILES):
+                pair[k] = scaled(k)
+            block = pair[pl.ds(0, TILES)].reshape(LANES, LANES)
+            products[pl.ds(0, TILES)] = dot_tall(block, tall[...]).reshape(TILES, 8, 2 * LANES)
             turned = []
             for k in range(TILES):
-                both = products[m * TILES + k]
+                both = products[k]
                 tile = both[:, :LANES] - sign * other_part(both[:, LANES:])
                 turned.append(tile_turn(tile, turn2[0, k], turn2[1, k]))
-            values = fft_up(turned, sign)
-            for t in range(TILES):
-                value = values[t]
-                if m == 1:
-                    extra[t] = value
-                    continue
-                if h == 0:
+            return fft_up(turned, sign)
+
+        values = lifted(lambda k: tables[3 * h + n, k] * spectra[h, k])
+        for t in range(TILES):
+            put4[n, h, 2 * t] = values[t][:4]
+            put4[n, h, 2 * t + 1] = values[t][4:]
+
+        def last_column(k):
+            wave = spectra[h, k]
+            return tables[2, k] * jnp.where(sublane() % 2 == 0, wave, roll_rows(wave, 1))
+
+        if h == 0:
+
+            @pl.when(row + col == 0)
+            def _():
+                if n == 0:
+                    for t, value in enumerate(lifted(last_column)):
+                        extra[t] = value
+                for t in range(TILES):
                     fixed = extra[t] if n == 0 else roll_rows(extra[t], 7)
-                    value = jnp.where(special, fixed, value)
-                put4[n, h, 2 * t] = value[:4]
-                put4[n, h, 2 * t + 1] = value[4:]
+                    value = jnp.where(sublane() % 4 == 2, fixed, two_blocks(put4.at[n, h], t))
+                    put4[n, h, 2 * t] = value[:4]
+                    put4[n, h, 2 * t + 1] = value[4:]
+
         send("row", put4.at[n, h], got4.at[n, h], SEND4 + 2 * n + h)
         got4[n, h, row] = put4[n, h, row]
 

time: 60.5 us -> 60.6 us (level)
  no operation moved by 1% of the time
where the time goes in v8:
time: 60.6 us; the launch traced here: 60.2 us
  Pallas kernels  59.6 us (98%)
  between operations  0.64 us (1%)
    pallas_call x1, Pallas kernels, on_device(): pl.pallas_call(kernel, name='section', out_shape=(shape, shape), in_specs...  58.8 us

profile of v8, /device:TPU:1, one launch (start us, length us, event | category | flops | bytes accessed | tf_op | source)
XLA Modules:
  0.0 60.2 jit_solution(15405429758461016125)
XLA Ops:
  0.6 58.8 %section.1 = (f32[16,8,256]{2,1,0:T(8,128)S(1)}, f32[16,8,256]{2,1,0:T(8,128)S(1)}) custom-call(f32[16,8,256]{2,1,0:T(8,128)} %bitcast.6, f32[16,8,256]{2,1,0:T(8,128)} %bitcast.7, bf16[4,512,512]{2,1,0:T(8,128)(2,1)} %constant.12.clone.wide_hbm, bf16[384,256]{1,0:T(8,128)(2,1)} %constant.13.clone.tall_hbm, f32[2,8,256]{2,1,0:T(8,128)} %constant.14.clone.turn1_hbm, ...), custom_call_target="tpu_custom_call" | custom-call | tf_op jit(solution)/shard_map/section/pallas_call | solution.py:603
  59.5 0.7 %store.1 = (f32[128,256]{1,0:T(8,128)}, f32[128,256]{1,0:T(8,128)}) custom-call(f32[128,256]{1,0:T(8,128)S(1)} %bitcast.4, f32[128,256]{1,0:T(8,128)S(1)} %bitcast.5), custom_call_target="tpu_custom_call" | custom-call | tf_op jit(solution)/shard_map/store/pallas_call | solution.py:660
